TPU v7x, 256 devices: a whole 4x4x8 slice. The times are simulated.
256 devices in a mesh: seq: 32 (over z, x_lo, core), fsdp: 8 (over x_hi, y).
Axes of the slice: x: 4 (x_hi: 2, x_lo: 2; x = x_hi * 2 + x_lo), y: 4, z: 8, core: 2. Of those that a mesh axis runs over, the one named last changes fastest.
Arguments:
- hidden_next: bfloat16 [8192, 8192], P('seq'), may hold values from -6 to 6
- values_next: bfloat16 [8192, 8192], P('seq', 'fsdp'), may hold values from -6 to 6
- seg_next: int32 [4], replicated, may hold values from 1 to 4096, 8192 in all
- proj_bc: bfloat16 [8192, 1024], P(('seq', 'fsdp')), may hold values from -0.09375 to 0.09375
- proj_dt: bfloat16 [8192, 128], P(('seq', 'fsdp')), may hold values from -0.0625 to 0.0625
- dt_bias: float32 [128], replicated, may hold values from -4 to -2.5
- decay_rate: float32 [128], replicated, may hold values from 0 to 1, as said below
- skip_gain: float32 [128], replicated, may hold values from 0.5 to 1.5
- bc_prev: bfloat16 [8192, 1024], P('seq'), may hold values from -4 to 4
- dt_prev: float32 [8192, 128], P('seq', 'fsdp'), may hold values from 0.01 to 0.3
- seg_prev: int32 [4], replicated, may hold values from 1 to 4096, 8192 in all
- grad_prev: bfloat16 [8192, 8192], P('seq', 'fsdp'), may hold values from -6 to 6
Outputs:
- out_next: bfloat16 [8192, 8192], P('seq', 'fsdp')
- grad_values: bfloat16 [8192, 8192], P('seq', 'fsdp')
Inputs may be any that keep to these rules, and one draw needn't show every extreme that they name: `seg_next`: lengths of the rollout's 4 segments in order, summing to 8192. `seg_prev`: lengths of the rollout's 4 segments in order, summing to 8192. `decay_rate`: positive.
All inputs are finite; a program needn't handle non-finite values.
Results may differ from a plain program's by a relative error of at most 0.0064.
Values may be sent and summed in bfloat16 or wider, within the bound.
No kernel may reach another device: no remote copies, remote signals or barrier semaphores. Data moves between devices by JAX's collectives and lax.ppermute only.
A program may use at most 128 MiB of HBM per device.

v0:
```python
import jax
import jax.numpy as jnp
from jax import lax
from jax.sharding import Mesh
from jax.sharding import PartitionSpec as P

GW = 4
SPAN = 128
SEQ = ("seq_0", "seq_1", "seq_2")
SEQ_FSDP = ("seq_0", "seq_1", "seq_2", "fsdp")


def in_one_piece(arrays, axis, dim, along):
    widths = [a.shape[along] for a in arrays]
    both = jnp.concatenate(arrays, axis=along)
    whole = lax.all_gather(both, axis, axis=dim, tiled=True)
    return tuple(jnp.split(whole, [sum(widths[:k]) for k in range(1, len(widths))], axis=along))


def filled_with(array, identity):
    return jax.tree.map(
        lambda a, e: jnp.broadcast_to(jnp.asarray(e, a.dtype), a.shape), array, identity
    )


def prefix_by_axis(array, axes, combine, identity, reverse):
    before = start = filled_with(array, identity)
    so_far = array
    for axis in reversed(axes):
        size, index = (lax.axis_size(axis), lax.axis_index(axis))
        pieces = jax.tree.map(lambda part: lax.all_gather(part, axis), so_far)
        inside, so_far = (start, start)
        for k in reversed(range(size)) if reverse else range(size):
            passed = k > index if reverse else k < index
            so_far = combine(so_far, jax.tree.map(lambda part: part[k], pieces))
            inside = jax.tree.map(lambda new, old: jnp.where(passed, new, old), so_far, inside)
        before = combine(inside, before)
    return before


def joined(earlier, later):
    return (earlier[0] * later[0], later[0][:, None] * earlier[1] + later[1])


def segment_marks(lengths, offset, length):
    bounds = jnp.cumsum(lengths)[:-1]
    places = offset + jnp.arange(length + 1, dtype=jnp.int32) - 1
    return jnp.sum((bounds[None, :] <= places[:, None]).astype(jnp.int32), axis=1)


def pick_groups(bc_rows, first_group, groups_dev, nblocks):
    tokens_dev, width_all = bc_rows.shape
    state_dim = width_all // (2 * GW)
    halves = bc_rows.reshape(tokens_dev, 2, GW, state_dim)
    picked = lax.dynamic_slice_in_dim(halves, first_group, groups_dev, 2)
    b_vectors = picked[:, 0].reshape(nblocks, tokens_dev // nblocks, groups_dev, state_dim)
    c_vectors = picked[:, 1].reshape(nblocks, tokens_dev // nblocks, groups_dev, state_dim)
    return (b_vectors, c_vectors)


def block_parts(b_vectors, c_vectors, dt_blocks, marks_all, decay_local):
    nblocks, span_len, groups, state_dim = b_vectors.shape
    heads_dev = dt_blocks.shape[2]
    segment = marks_all[1:].reshape(nblocks, span_len)
    before = marks_all[:-1].reshape(nblocks, span_len)[:, 0]
    cumulative = jnp.cumsum(-dt_blocks * decay_local, axis=1)
    final_cum = cumulative[:, -1]
    places = jnp.arange(span_len)
    linked = (segment[:, :, None] == segment[:, None, :]) & (places[:, None] >= places[None, :])
    scores = jnp.einsum("ktgn,ksgn->kgts", c_vectors, b_vectors, preferred_element_type=jnp.float32)
    by_head = jnp.swapaxes(cumulative, 1, 2)
    spread = by_head[:, :, :, None] - by_head[:, :, None, :]
    decays = jnp.exp(jnp.where(linked[:, None], spread, -jnp.inf))
    weighted = (decays * jnp.swapaxes(dt_blocks, 1, 2)[:, :, None, :]).reshape(
        nblocks, groups, heads_dev // groups, span_len, span_len
    )
    mixing = (
        (weighted * scores[:, :, None])
        .reshape(nblocks, heads_dev, span_len, span_len)
        .astype(jnp.bfloat16)
    )
    keep_final = (segment == segment[:, -1:]).astype(jnp.float32)
    linked_in = (segment == before[:, None]).astype(jnp.float32)
    send_factor = keep_final[:, :, None] * jnp.exp(final_cum[:, None, :] - cumulative) * dt_blocks
    read_factor = linked_in[:, :, None] * jnp.exp(cumulative)
    carry_decay = (segment[:, -1] == before).astype(jnp.float32)[:, None] * jnp.exp(final_cum)
    return (mixing, send_factor, read_factor, carry_decay)


def outer_sum(values, vectors):
    nblocks, span_len, heads_dev, head_dim = values.shape
    groups = vectors.shape[2]
    grouped = values.reshape(nblocks, span_len, groups, heads_dev // groups, head_dim)
    result = jnp.einsum("ksgqp,ksgn->kgqpn", grouped, vectors, preferred_element_type=jnp.float32)
    return result.reshape(nblocks, heads_dev, head_dim * vectors.shape[3])


def read_state(state_now, vectors, factor):
    nblocks, heads_dev, head_dim, state_dim = state_now.shape
    groups = vectors.shape[2]
    grouped = state_now.reshape(nblocks, groups, heads_dev // groups, head_dim, state_dim)
    result = jnp.einsum(
        "kgqpn,ktgn->ktgqp", grouped, vectors.astype(jnp.float32), precision=lax.Precision.HIGHEST
    )
    return result.reshape(nblocks, vectors.shape[1], heads_dev, head_dim) * factor[:, :, :, None]


def body(
    hidden_next,
    values_next,
    seg_next,
    proj_bc,
    proj_dt,
    dt_bias,
    decay_rate,
    skip_gain,
    bc_prev,
    dt_prev,
    seg_prev,
    grad_prev,
):
    tokens_dev = hidden_next.shape[0]
    bc_width = proj_bc.shape[1]
    heads_all = proj_dt.shape[1]
    fsdp_count = lax.axis_size("fsdp")
    fsdp_place = lax.axis_index("fsdp")
    heads_dev = heads_all // fsdp_count
    head_dim = values_next.shape[1] // heads_dev
    state_dim = bc_width // (2 * GW)
    flat_size = head_dim * state_dim
    per_group = heads_all // GW
    groups_dev = max(1, heads_dev // per_group)
    first_head = fsdp_place * heads_dev
    first_group = first_head // per_group
    rows_dev = proj_bc.shape[0]
    seq_count = lax.axis_size(SEQ)
    arranged = hidden_next.reshape(tokens_dev, seq_count, fsdp_count, rows_dev)
    owned = lax.dynamic_slice_in_dim(arranged, fsdp_place, 1, 2).reshape(
        tokens_dev, seq_count * rows_dev
    )
    pieces = in_one_piece((proj_bc, proj_dt), SEQ, 0, 1)
    bc_sum, dt_sum = lax.psum(
        (
            jnp.dot(owned, pieces[0], preferred_element_type=jnp.float32),
            jnp.dot(owned, pieces[1], preferred_element_type=jnp.float32),
        ),
        "fsdp",
    )
    bc_next = bc_sum.astype(jnp.bfloat16)
    bias_local = lax.dynamic_slice_in_dim(dt_bias, first_head, heads_dev, 0)
    decay_local = lax.dynamic_slice_in_dim(decay_rate, first_head, heads_dev, 0)
    skip_local = lax.dynamic_slice_in_dim(skip_gain, first_head, heads_dev, 0)
    dt_next = jax.nn.softplus(
        lax.dynamic_slice_in_dim(dt_sum, first_head, heads_dev, 1) + bias_local
    )
    offset = lax.axis_index(SEQ) * tokens_dev
    nblocks = tokens_dev // SPAN
    unit_decay = jnp.ones((heads_dev,), jnp.float32)
    zero_state = jnp.zeros((heads_dev, flat_size), jnp.float32)
    inputs = values_next.reshape(nblocks, SPAN, heads_dev, head_dim)
    marks_next = segment_marks(seg_next, offset, tokens_dev)
    b_vectors, c_vectors = pick_groups(bc_next, first_group, groups_dev, nblocks)
    mixing, send_factor, read_factor, carry_decay = block_parts(
        b_vectors, c_vectors, dt_next.reshape(nblocks, SPAN, heads_dev), marks_next, decay_local
    )
    scaled = (inputs.astype(jnp.float32) * send_factor[:, :, :, None]).astype(jnp.bfloat16)
    local_sums = outer_sum(scaled, b_vectors)
    summary = (unit_decay, zero_state)
    for block_id in range(nblocks):
        summary = joined(summary, (carry_decay[block_id], local_sums[block_id]))
    arrived = prefix_by_axis((summary[0], summary[1]), SEQ, joined, (unit_decay, zero_state), False)
    state_now = arrived[1]
    starts_list = []
    for block_id in range(nblocks):
        starts_list.append(state_now)
        if block_id + 1 < nblocks:
            state_now = carry_decay[block_id][:, None] * state_now + local_sums[block_id]
    entering = jnp.stack(starts_list).reshape(nblocks, heads_dev, head_dim, state_dim)
    inside = jnp.einsum("khts,kshp->kthp", mixing, inputs, preferred_element_type=jnp.float32)
    output = (
        inside
        + read_state(entering, c_vectors, read_factor)
        + skip_local[:, None] * inputs.astype(jnp.float32)
    )
    out_next = output.astype(jnp.bfloat16).reshape(tokens_dev, heads_dev * head_dim)
    grads_in = grad_prev.reshape(nblocks, SPAN, heads_dev, head_dim)
    marks_prev = segment_marks(seg_prev, offset, tokens_dev)
    b_back, c_back = pick_groups(bc_prev, first_group, groups_dev, nblocks)
    mixing_back, send_back, read_back, carry_back = block_parts(
        b_back, c_back, dt_prev.reshape(nblocks, SPAN, heads_dev), marks_prev, decay_local
    )
    scaled_back = (grads_in.astype(jnp.float32) * read_back[:, :, :, None]).astype(jnp.bfloat16)
    local_back = outer_sum(scaled_back, c_back)
    summary_back = (unit_decay, zero_state)
    for block_id in reversed(range(nblocks)):
        summary_back = joined(summary_back, (carry_back[block_id], local_back[block_id]))
    arrived_back = prefix_by_axis(
        (summary_back[0], summary_back[1]), SEQ, joined, (unit_decay, zero_state), True
    )
    state_back = arrived_back[1]
    ends_list = [zero_state] * nblocks
    for block_id in reversed(range(nblocks)):
        ends_list[block_id] = state_back
        if block_id > 0:
            state_back = carry_back[block_id][:, None] * state_back + local_back[block_id]
    leaving = jnp.stack(ends_list).reshape(nblocks, heads_dev, head_dim, state_dim)
    inside_back = jnp.einsum(
        "khts,kthp->kshp", mixing_back, grads_in, preferred_element_type=jnp.float32
    )
    gradient = (
        inside_back
        + read_state(leaving, b_back, send_back)
        + skip_local[:, None] * grads_in.astype(jnp.float32)
    )
    grad_values = gradient.astype(jnp.bfloat16).reshape(tokens_dev, heads_dev * head_dim)
    return (out_next, grad_values)


def solution(mesh):
    split = Mesh(
        mesh.devices.reshape(8, 2, 2, mesh.shape["fsdp"]), ("seq_0", "seq_1", "seq_2", "fsdp")
    )
    in_specs = (
        P(SEQ, None),
        P(SEQ, "fsdp"),
        P(),
        P(SEQ_FSDP, None),
        P(SEQ_FSDP, None),
        P(),
        P(),
        P(),
        P(SEQ, None),
        P(SEQ, "fsdp"),
        P(),
        P(SEQ, "fsdp"),
    )
    out_specs = (P(SEQ, "fsdp"), P(SEQ, "fsdp"))
    return jax.shard_map(body, mesh=split, in_specs=in_specs, out_specs=out_specs, check_vma=False)
```

profile of v0, /device:TPU:1, one launch (start us, length us, event | category | flops | bytes accessed | tf_op | source)
XLA Modules:
  0.0 394.7 jit_solution(7305835161646682125)
XLA Ops:
  10.5 6.5 %copy.114 = bf16[256,8192]{0,1:T(8,128)(2,1)} copy(bf16[256,8192]{1,0:T(8,128)(2,1)} %param.12) | data formatting | bytes 8388608 | tf_op args[0]
  24.6 54.7 %all-gather.14.cloned.1.call-done = bf16[1024,1152]{1,0:T(8,128)(2,1)} async-done(((bf16[32,1152]{1,0:T(8,128)(2,1)}), bf16[1024,1152]{1,0:T(8,128)(2,1)}) %all-gather.14.cloned.1.call-update) | async-done | bytes 2359312 | tf_op jit(solution)/shard_map/all_gather | solution.py:16
  81.3 2.3 fusion
  83.6 67.7 %all-reduce.4 = bf16[256,1024]{1,0:T(8,128)(2,1)S(1)} all-reduce(f32[256,1024]{1,0:T(8,128)S(1)} %fusion), channel_id=1, replica_groups=mesh['seq_0'=8,'seq_1'=2,'seq_2'=2,'fsdp'=8] {'fsdp'}, use_global_device_ids=true, to_apply=%region_4.5 | all-reduce | flops 262144 | bytes 1572864 | tf_op jit(solution)/shard_map/psum | solution.py:142
  153.0 13.6 %all-reduce.3.cloned.1.call-done = f32[256,128]{0,1:T(8,128)} async-done(((f32[256,128]{0,1:T(8,128)}), f32[256,128]{0,1:T(8,128)}) %all-reduce.3.cloned.1.call-update) | async-done | bytes 131088 | tf_op jit(solution)/shard_map/psum | solution.py:142
  172.2 7.2 %all-gather.3 = f32[2,1,16]{2,1,0:T(1,128)S(1)} all-gather(f32[1,1,16]{2,1,0:T(1,128)S(1)} %get-tuple-element.64), channel_id=1, replica_groups=mesh['seq_0'=8,'seq_1'=2,'seq_2'=2,'fsdp'=8] {'seq_2'}, dimensions={0}, use_global_device_ids=true | all-gather | bytes 192 | tf_op jit(solution)/shard_map/all_gather | solution.py:31
  179.9 3.1 all-gather.4
  185.1 3.1 all-gather
  188.2 3.1 all-gather.1
  194.0 2.1 slice_add_fusion.10
  196.2 12.1 %all-gather.16.cloned.1.call-done = f32[2,16,8192]{2,1,0:T(8,128)} async-done(((f32[1,16,8192]{2,1,0:T(8,128)}), f32[2,16,8192]{2,1,0:T(8,128)}) %all-gather.16.cloned.1.call-update) | async-done | bytes 1048592 | tf_op jit(solution)/shard_map/all_gather | solution.py:31
  208.3 2.1 slice_add_fusion.22
  210.5 26.8 %all-gather.24.cloned.1.call-done = f32[2,16,8192]{2,1,0:T(8,128)} async-done(((f32[1,16,8192]{2,1,0:T(8,128)}), f32[2,16,8192]{2,1,0:T(8,128)}) %all-gather.24.cloned.1.call-update) | async-done | bytes 1048592 | tf_op jit(solution)/shard_map/all_gather | solution.py:31
  237.4 2.2 slice_add_fusion.8
  239.7 27.3 %all-gather.18.cloned.1.call-done = f32[2,16,8192]{2,1,0:T(8,128)} async-done(((f32[1,16,8192]{2,1,0:T(8,128)}), f32[2,16,8192]{2,1,0:T(8,128)}) %all-gather.18.cloned.1.call-update) | async-done | bytes 1048592 | tf_op jit(solution)/shard_map/all_gather | solution.py:31
  266.9 2.1 slice_add_fusion.20
  273.8 13.9 %all-gather.5 = f32[8,1,16]{2,1,0:T(1,128)S(1)} all-gather(f32[1,1,16]{2,1,0:T(1,128)S(1)} %copy-done.55), channel_id=1, replica_groups=mesh['seq_0'=8,'seq_1'=2,'seq_2'=2,'fsdp'=8] {'seq_0'}, dimensions={0}, use_global_device_ids=true | all-gather | bytes 576 | tf_op jit(solution)/shard_map/all_gather | solution.py:31
  287.7 12.6 %all-gather.2 = f32[8,1,16]{2,1,0:T(1,128)S(1)} all-gather(f32[1,1,16]{2,1,0:T(1,128)S(1)} %get-tuple-element.67), channel_id=1, replica_groups=mesh['seq_0'=8,'seq_1'=2,'seq_2'=2,'fsdp'=8] {'seq_0'}, dimensions={0}, use_global_device_ids=true | all-gather | bytes 576 | tf_op jit(solution)/shard_map/all_gather | solution.py:31
  302.2 2.7 convolution_bitcast_fusion.1
  304.9 19.6 %all-gather.26.cloned.1.call-done = f32[8,16,8192]{2,1,0:T(8,128)} async-done(((f32[1,16,8192]{2,1,0:T(8,128)}), f32[8,16,8192]{2,1,0:T(8,128)}) %all-gather.26.cloned.1.call-update) | async-done | bytes 4194320 | tf_op jit(solution)/shard_map/all_gather | solution.py:31
  324.6 3.2 add_bitcast_fusion
  331.6 2.6 reshape.987
  334.2 46.1 %all-gather.20.cloned.1.call-done = f32[8,16,8192]{2,1,0:T(8,128)} async-done(((f32[1,16,8192]{2,1,0:T(8,128)}), f32[8,16,8192]{2,1,0:T(8,128)}) %all-gather.20.cloned.1.call-update) | async-done | bytes 4194320 | tf_op jit(solution)/shard_map/all_gather | solution.py:31
  380.3 3.2 add_bitcast_fusion.1
  (225 shorter events, 39.8 us)
Async XLA Ops:
  7.2 72.2 %all-gather.14.cloned.1.call-start = ((), (), s32[]{:S(2)}) async-start(), calls=%async_computation | async-start | bytes 2433024 | tf_op jit(solution)/shard_map/all_gather | solution.py:16
  8.7 157.9 %all-reduce.3.cloned.1.call-start = ((), (), s32[]{:S(2)}) async-start(), calls=%async_computation.1 | async-start | bytes 262144 | tf_op jit(solution)/shard_map/psum | solution.py:142
  81.2 112.8 %all-gather.22.cloned.1.call-start = ((), (), s32[]{:S(2)}) async-start(), calls=%async_computation.5 | async-start | bytes 1572864 | tf_op jit(solution)/shard_map/all_gather | solution.py:31
  172.1 36.2 %all-gather.16.cloned.1.call-start = ((), (), s32[]{:S(2)}) async-start(), calls=%async_computation.2 | async-start | bytes 1572864 | tf_op jit(solution)/shard_map/all_gather | solution.py:31
  192.8 44.5 %all-gather.24.cloned.1.call-start = ((), (), s32[]{:S(2)}) async-start(), calls=%async_computation.6 | async-start | bytes 1572864 | tf_op jit(solution)/shard_map/all_gather | solution.py:31
  193.5 43.9 %copy-start.30 = (f32[16]{0:T(128)}, f32[16]{0:T(128)S(1)}, u32[]{:S(2)}) copy-start(f32[16]{0:T(128)S(1)} %get-tuple-element.61) | copy-start | bytes 196
  194.0 72.9 %copy-start.26 = (f32[16]{0:T(128)}, f32[16]{0:T(128)S(1)}, u32[]{:S(2)}) copy-start(f32[16]{0:T(128)S(1)} %get-tuple-element.70) | copy-start | bytes 196
  194.0 43.3 %copy-start.36 = (f32[16]{0:T(128)S(1)}, f32[16]{0:T(128)}, u32[]{:S(2)}) copy-start(f32[16]{0:T(128)} %get-tuple-element.59) | copy-start | bytes 196
  196.2 70.8 %all-gather.18.cloned.1.call-start = ((), (), s32[]{:S(2)}) async-start(), calls=%async_computation.3 | async-start | bytes 1572864 | tf_op jit(solution)/shard_map/all_gather | solution.py:31
  210.5 114.1 %all-gather.26.cloned.1.call-start = ((), (), s32[]{:S(2)}) async-start(), calls=%async_computation.7 | async-start | bytes 4718592 | tf_op jit(solution)/shard_map/all_gather | solution.py:31
  237.4 33.2 %copy-start.11 = (bf16[256,1,1,128]{3,2,1,0:T(2,128)(2,1)S(1)}, bf16[256,1,1,128]{3,2,1,0:T(2,128)(2,1)}, u32[]{:S(2)}) copy-start(bf16[256,1,1,128]{3,2,1,0:T(2,128)(2,1)} %get-tuple-element.24) | copy-start | bytes 196612
  237.4 33.2 %copy-start.10 = (bf16[256,1,1,128]{3,2,1,0:T(2,128)(2,1)S(1)}, bf16[256,1,1,128]{3,2,1,0:T(2,128)(2,1)}, u32[]{:S(2)}) copy-start(bf16[256,1,1,128]{3,2,1,0:T(2,128)(2,1)} %get-tuple-element.82) | copy-start | bytes 196612
  237.4 33.3 %copy-start.5 = (bf16[256,1,1,128]{3,0,2,1:T(8,128)(2,1)S(1)}, bf16[256,1,1,128]{3,0,2,1:T(8,128)(2,1)}, u32[]{:S(2)}) copy-start(bf16[256,1,1,128]{3,0,2,1:T(8,128)(2,1)} %copy-done.4) | copy-start | bytes 196612
  239.6 32.8 %copy-start.14 = (f32[2,128,16]{2,1,0:T(8,128)S(1)}, f32[2,128,16]{2,1,0:T(8,128)}, u32[]{:S(2)}) copy-start(f32[2,128,16]{2,1,0:T(8,128)} %get-tuple-element.30) | copy-start | bytes 49156
  239.6 34.2 %copy-start.55 = (f32[1,1,16]{2,1,0:T(1,128)S(1)}, f32[1,1,16]{2,1,0:T(1,128)}, u32[]{:S(2)}) copy-start(f32[1,1,16]{2,1,0:T(1,128)} %get-tuple-element.58) | copy-start | bytes 196
  239.6 140.7 %all-gather.20.cloned.1.call-start = ((), (), s32[]{:S(2)}) async-start(), calls=%async_computation.4 | async-start | bytes 4718592 | tf_op jit(solution)/shard_map/all_gather | solution.py:31
  329.8 50.5 %copy-start = (f32[2,16,8192]{2,1,0:T(8,128)S(1)}, f32[2,16,8192]{2,1,0:T(8,128)}, u32[]{:S(2)}) copy-start(f32[2,16,8192]{2,1,0:T(8,128)} %all-gather.16.cloned.1.call-done) | copy-start | bytes 3145732
  329.8 50.5 %copy-start.25 = (f32[16]{0:T(128)S(1)}, f32[16]{0:T(128)}, u32[]{:S(2)}) copy-start(f32[16]{0:T(128)} %copy-done.24) | copy-start | bytes 196
  329.8 50.5 %copy-start.27 = (f32[16]{0:T(128)S(1)}, f32[16]{0:T(128)}, u32[]{:S(2)}) copy-start(f32[16]{0:T(128)} %copy-done.26) | copy-start | bytes 196
  329.8 50.5 %copy-start.33 = (f32[16]{0:T(128)S(1)}, f32[16]{0:T(128)}, u32[]{:S(2)}) copy-start(f32[16]{0:T(128)} %copy-done.32) | copy-start | bytes 196
  329.9 50.5 %copy-start.39 = (f32[16]{0:T(128)S(1)}, f32[16]{0:T(128)}, u32[]{:S(2)}) copy-start(f32[16]{0:T(128)} %copy-done.38) | copy-start | bytes 196
  329.9 50.5 %copy-start.48 = (f32[16]{0:T(128)S(1)}, f32[16]{0:T(128)}, u32[]{:S(2)}) copy-start(f32[16]{0:T(128)} %get-tuple-element.75) | copy-start | bytes 196
  329.9 50.5 %copy-start.50 = (f32[16]{0:T(128)S(1)}, f32[16]{0:T(128)}, u32[]{:S(2)}) copy-start(f32[16]{0:T(128)} %get-tuple-element.18) | copy-start | bytes 196
  329.9 50.5 %copy-start.51 = (f32[16]{0:T(128)S(1)}, f32[16]{0:T(128)}, u32[]{:S(2)}) copy-start(f32[16]{0:T(128)} %get-tuple-element.19) | copy-start | bytes 196
  (44 other events, 685.8 us)
Sparse Core Ops, SparseCore 0:
  10.4 68.8 all-gather.13
  82.5 84.1 all-reduce.2
  172.3 18.1 all-gather.21
  192.9 15.3 all-gather.15
  210.5 26.7 all-gather.23
  239.6 27.3 all-gather.17
  268.7 55.7 all-gather.25
  326.9 53.3 all-gather.19
where the time goes:
time: 395 us
  waiting for transfers between devices  200 us (51%)
  blocking collectives  111 us (28%)
  other arithmetic  30.4 us (8%)
  local copies, waits for them, and re-layouts  26.2 us (7%)
  between operations  15 us (4%)
  matrix products  11.8 us (3%)
    all_gather x6, waiting for transfers between devices, prefix_by_axis(): pieces = jax.tree.map(lambda part: lax.all_gather(part, axis), so_far)  132 us
    psum x1, blocking collectives, body(): lax.psum((jnp.dot(owned, pieces[0], preferred_element_type=jnp.float32),...  67.7 us
    all_gather x1, waiting for transfers between devices, in_one_piece(): whole = lax.all_gather(both, axis, axis=dim, tiled=True)  54.7 us
    all_gather x6, blocking collectives, prefix_by_axis(): pieces = jax.tree.map(lambda part: lax.all_gather(part, axis), so_far)  42.9 us
    unnamed x134, local copies, waits for them, and re-layouts  15.8 us
    psum x1, waiting for transfers between devices, body(): lax.psum((jnp.dot(owned, pieces[0], preferred_element_type=jnp.float32),...  13.6 us
    add x6, other arithmetic, joined(): return (earlier[0] * later[0], later[0][:, None] * earlier[1] + later[1])  11 us
  transfers between devices with their start and end apart: 8, of which 7 were waited for; matrix products, arithmetic and copies ran while one was open for 13% of the time, Pallas kernels for 0%

commit v1 on v0

v1 whole, which is shorter than its diff:
```python
import functools
import jax
import jax.numpy as jnp
from jax import lax
from jax.experimental import pallas as pl
from jax.experimental.pallas import tpu as pltpu
from jax.sharding import Mesh
from jax.sharding import PartitionSpec as P

SEQ = ("z", "xl", "c")
FSDP = ("xh", "y")
BF = jnp.bfloat16
F32 = jnp.float32
T = 256
HEADS = 16
PAIRS = HEADS // 2
NEG = -1e30
VM = pl.BlockSpec(memory_space=pltpu.VMEM)
SM = pl.BlockSpec(memory_space=pltpu.SMEM)


def call(kernel, outs, name, n_smem, args, flops=10_000_000, nbytes=1_000_000):
    return pl.pallas_call(
        kernel,
        out_shape=outs,
        in_specs=[SM] * n_smem + [VM] * (len(args) - n_smem),
        out_specs=jax.tree.map(lambda _: VM, outs),
        name=name,
        cost_estimate=pl.CostEstimate(flops=flops, bytes_accessed=nbytes, transcendentals=0),
    )(*args)


def sds(shape, dtype):
    return jax.ShapeDtypeStruct(shape, dtype)


def lanes(shape):
    return lax.broadcasted_iota(jnp.int32, shape, len(shape) - 1)


def rows(shape):
    return lax.broadcasted_iota(jnp.int32, shape, len(shape) - 2)


def k_columns(sc, bc_ref, dt_ref, out_ref):
    me = sc[7]
    lane = lanes((32, 128))
    low = lane < 64
    for j in range(4):
        b = bc_ref[:, 128 * j : 128 * j + 128].astype(F32)
        c = bc_ref[:, 512 + 128 * j : 640 + 128 * j].astype(F32)
        out_ref[2 * j, 0:32] = jnp.where(low, b, pltpu.roll(c, 64, 1)).astype(BF)
        out_ref[2 * j + 1, 0:32] = jnp.where(low, pltpu.roll(b, 64, 1), c).astype(BF)
    d = dt_ref[...].astype(F32)
    mine = lane // 16 == me
    for k in range(8):
        out_ref[k, 32:64] = jnp.where(mine, pltpu.roll(d, (16 * (me - k)) & 127, 1), 0.0).astype(BF)


def k_rows(rec_ref, out_ref):
    total = jnp.zeros((32, 128), F32)
    for k in range(8):
        out_ref[32 * k : 32 * k + 32] = rec_ref[k, 0:32]
        total = total + rec_ref[k, 32:64].astype(F32)
    out_ref[256:288] = total.astype(BF)


def k_quad(sc, own, other_x, other_c, other_xc, out_ref):
    c, x = sc[4], sc[5]
    out_ref[2 * x + c] = own[...]
    out_ref[2 * (1 - x) + c] = other_x[...]
    out_ref[2 * x + 1 - c] = other_c[...]
    out_ref[2 * (1 - x) + 1 - c] = other_xc[...]


def k_project(sc, hid, q0, r1, g1, r2, g2, r3, g3, h_own, h_other, y_ref, dt_ref):
    c, z = sc[4], sc[6]
    sign = 1 - 2 * c
    spread = (lanes((T, 128)) // 16) == (rows((T, 128)) // 32)

    def block(part):
        packed = part[256:288]
        tall = jnp.concatenate([packed] * 8, axis=0)
        return jnp.concatenate([part[0:256], jnp.where(spread, tall, jnp.zeros_like(tall))], axis=1)

    def times(off, parts):
        width = 256 * len(parts)
        left = hid[:, pl.ds(pl.multiple_of(off, 256), width)]
        right = jnp.concatenate([block(p) for p in parts], axis=0)
        return jnp.dot(left, right, preferred_element_type=F32)

    acc = times(1024 * z, [q0[b] for b in range(4)])
    for r, (up, down) in enumerate(((r1, g1), (r2, g2), (r3, g3)), 1):
        acc = acc + times(1024 * ((z - sign * r) & 7), [up[b] for b in range(4)])
        acc = acc + times(1024 * ((z + sign * r) & 7), [down[b] for b in range(4)])
    far = 1024 * ((z + 4) & 7)
    acc = acc + times(far + 512 * c, [h_own[b] for b in range(2)])
    acc = acc + times(far + 512 * (1 - c), [h_other[b] for b in range(2)])
    y_ref[...] = acc[:, 0:128].astype(BF)
    d = acc[:, 128:256]
    for shift in (16, 32, 64):
        d = d + pltpu.roll(d, shift, 1)
    dt_ref[...] = d


def gather_weights(sc, proj_bc, proj_dt):
    send = call(k_columns, sds((8, 64, 128), BF), "columns", 1, (sc, proj_bc, proj_dt))
    got = lax.all_to_all(send, FSDP, 0, 0, tiled=False)
    own = call(k_rows, sds((288, 128), BF), "rows", 0, (got,))
    swap = [(0, 1), (1, 0)]
    other_x = lax.ppermute(own, "xl", swap)
    other_c = lax.ppermute(own, "c", swap)
    other_xc = lax.ppermute(other_x, "c", swap)
    quad = call(k_quad, sds((4, 288, 128), BF), "quad", 1, (sc, own, other_x, other_c, other_xc))
    ring = [(2 * z, 2 * ((z + 1) % 8)) for z in range(8)] + [(2 * z + 1, 2 * ((z - 1) % 8) + 1) for z in range(8)]
    got, swapped, now = [], [], quad
    for _ in range(3):
        now = lax.ppermute(now, ("z", "c"), ring)
        got.append(now)
        swapped.append(lax.ppermute(now, "c", swap))
    half = lax.dynamic_slice_in_dim(now, 2 * lax.axis_index("c"), 2, 0)
    far = lax.ppermute(half, ("z", "c"), ring)
    far_other = lax.ppermute(far, "c", swap)
    return quad, got[0], swapped[0], got[1], swapped[1], got[2], swapped[2], far, far_other


def segment_of(sc, place):
    return (
        (place >= sc[0]).astype(jnp.int32) + (place >= sc[1]).astype(jnp.int32) + (place >= sc[2]).astype(jnp.int32)
    )


def scalar_segment(sc, place):
    one, none = jnp.int32(1), jnp.int32(0)
    return sum((jnp.where(place >= sc[k], one, none) for k in range(3)), none)


def expand(factor, j, low):
    a = jnp.broadcast_to(factor[:, 2 * j : 2 * j + 1], (T, 128))
    b = jnp.broadcast_to(factor[:, 2 * j + 1 : 2 * j + 2], (T, 128))
    return jnp.where(low, a, b)


def local_part(reverse, sc, dt, decay, b, c, val_ref, outs, scratch):
    keep_ref, send_ref, cum_ref, cumt_ref, dtt_ref, late_ref = outs
    offset, core = sc[3], sc[4]
    before, last = scalar_segment(sc, offset - 1), scalar_segment(sc, offset + T - 1)
    dt_t = jnp.transpose(dt)[0:HEADS]
    x = -jnp.transpose(dt * decay)[0:HEADS]
    lane = lanes((HEADS, T))
    for shift in (1, 2, 4, 8, 16, 32, 64, 128):
        x = x + jnp.where(lane >= shift, pltpu.roll(x, shift, 1), 0.0)
    cum_t = x
    cum = jnp.transpose(jnp.concatenate([cum_t] * 8, axis=0))
    final = cum[T - 1 : T]
    place = offset + rows((T, 128))
    seg = segment_of(sc, place)
    send = jnp.where(seg == last, jnp.exp(final - cum) * dt, 0.0)
    read = jnp.where(seg == before, jnp.exp(cum), 0.0)
    early, late = (read, send) if reverse else (send, read)
    cum_ref[...] = cum
    cumt_ref[...] = cum_t
    dtt_ref[...] = dt_t
    late_ref[...] = late
    low = lanes((T, 128)) < 64
    side = c if reverse else b
    for j in range(PAIRS):
        v = val_ref[:, 128 * j : 128 * j + 128].astype(F32)
        scaled = (v * expand(early, j, low)).astype(BF)
        out = lax.dot_general(scaled, side, (((0,), (0,)), ((), ())), preferred_element_type=F32)
        scratch[j // 4, 128 * (j % 4) : 128 * (j % 4) + 128] = out.astype(BF)
    a = jnp.broadcast_to(jnp.exp(cum_t[:, T - 1 : T]), (HEADS, 128))
    a = jnp.where(last == before, a, 0.0)
    high = a.astype(BF).astype(F32)
    rest = a - high
    for half in range(2):
        pick = slice(8 * half, 8 * half + 8)
        scratch[half, 512:528] = jnp.concatenate([high[pick], rest[pick]], axis=0).astype(BF)
    keep_ref[...] = scratch[core]
    send_ref[...] = scratch[1 - core]


def k_local_prev(sc, dt_ref, par, b_ref, c_ref, val_ref, *refs):
    local_part(True, sc, dt_ref[...], par[0:1], b_ref[...], c_ref[...], val_ref, refs[:6], refs[6])


def softplus(v):
    return jnp.maximum(v, 0.0) + jnp.log1p(jnp.exp(-jnp.abs(v)))


def k_local_next(sc, dt_ref, par, mine_ref, pair_ref, val_ref, *refs):
    outs, b_out, c_out, scratch = refs[:6], refs[6], refs[7], refs[8]
    odd = (sc[7] & 1) == 1
    mine, pair = mine_ref[...].astype(F32), pair_ref[...].astype(F32)
    lo, hi = jnp.where(odd, pair, mine), jnp.where(odd, mine, pair)
    low = lanes((T, 128)) < 64
    b = jnp.where(low, lo, pltpu.roll(hi, 64, 1)).astype(BF)
    c = jnp.where(low, pltpu.roll(lo, 64, 1), hi).astype(BF)
    b_out[...] = b
    c_out[...] = c
    dt = softplus(dt_ref[...] + par[1:2])
    local_part(False, sc, dt, par[0:1], b, c, val_ref, outs, scratch)


LOCAL_OUTS = (
    sds((528, 128), BF),
    sds((528, 128), BF),
    sds((T, 128), F32),
    sds((HEADS, T), F32),
    sds((HEADS, T), F32),
    sds((T, 128), F32),
)


def call_scratch(kernel, outs, name, n_smem, args, scratch, flops):
    return pl.pallas_call(
        kernel,
        out_shape=outs,
        in_specs=[SM] * n_smem + [VM] * (len(args) - n_smem),
        out_specs=jax.tree.map(lambda _: VM, outs),
        scratch_shapes=scratch,
        name=name,
        cost_estimate=pl.CostEstimate(flops=flops, bytes_accessed=2_000_000, transcendentals=0),
    )(*args)


def k_inside(reverse, sc, skip, cum_ref, cumt_ref, dtt_ref, b_ref, c_ref, val_ref, out_ref, bias_ref, score_ref):
    offset, first_head = sc[3], HEADS * sc[7]
    shape = (T, T)
    seg_r = segment_of(sc, offset + rows(shape))
    seg_l = segment_of(sc, offset + lanes(shape))
    causal = rows(shape) <= lanes(shape) if reverse else rows(shape) >= lanes(shape)
    bias_ref[...] = jnp.where((seg_r == seg_l) & causal, 0.0, NEG)
    one, two = (b_ref, c_ref) if reverse else (c_ref, b_ref)
    score_ref[...] = lax.dot_general(one[...], two[...], (((1,), (1,)), ((), ())), preferred_element_type=F32)
    low = lanes((T, 128)) < 64
    cum = cum_ref[...]
    for j in range(PAIRS):
        v = val_ref[:, 128 * j : 128 * j + 128]
        parts = []
        for h in (2 * j, 2 * j + 1):
            col = jnp.broadcast_to(cum[:, h : h + 1], shape)
            row = cumt_ref[h : h + 1]
            if reverse:
                spread = row - col
            else:
                spread = col - row
            decays = jnp.exp(spread + bias_ref[...])
            if reverse:
                mix = (decays * score_ref[...])
            else:
                mix = decays * dtt_ref[h : h + 1] * score_ref[...]
            parts.append(jnp.dot(mix.astype(BF), v, preferred_element_type=F32))
        inside = jnp.where(low, parts[0], parts[1])
        gain = jnp.where(low, skip[first_head + 2 * j], skip[first_head + 2 * j + 1])
        if reverse:
            dt = jnp.transpose(jnp.concatenate([dtt_ref[...]] * 8, axis=0)) if j == 0 else dt
            inside = inside * expand(dt, j, low)
        out_ref[:, 128 * j : 128 * j + 128] = inside + gain * v.astype(F32)


def k_final(sc, base_ref, late_ref, side_ref, keep_ref, got_ref, out_ref, scratch):
    core = sc[4]
    scratch[core] = keep_ref[...]
    scratch[1 - core] = got_ref[...]
    low = lanes((T, 128)) < 64
    late = late_ref[...]
    for j in range(PAIRS):
        st = scratch[j // 4, 128 * (j % 4) : 128 * (j % 4) + 128]
        seen = lax.dot_general(side_ref[...], st, (((1,), (1,)), ((), ())), preferred_element_type=F32)
        at = slice(128 * j, 128 * j + 128)
        out_ref[:, at] = (base_ref[:, at] + expand(late, j, low) * seen).astype(BF)


def decays_of(tail):
    t = tail.astype(F32)
    return t[0:8] + t[8:16]


def tail_of(a):
    high = a.astype(BF).astype(F32)
    return jnp.concatenate([high, a - high], axis=0).astype(BF)


def per_row(a, heads):
    return jnp.concatenate([jnp.broadcast_to(a[h : h + 1], (64, 128)) for h in range(heads)], axis=0)


def quarter_rows(a, which):
    return per_row(jnp.where(which == 0, a[0:4], a[4:8]), 4)


def first_of(reverse, bit):
    return (bit == 1) if reverse else (bit == 0)


def k_core(reverse, sc, own, got, keep_ref, send_ref, scratch):
    core, x = sc[4], sc[5]
    mine_first = first_of(reverse, core)
    so, sg = own[0:512].astype(F32), got[0:512].astype(F32)
    ao, ag = decays_of(own[512:528]), decays_of(got[512:528])
    first, second = jnp.where(mine_first, so, sg), jnp.where(mine_first, sg, so)
    a_second = jnp.where(mine_first, ag, ao)
    joined = (second + per_row(a_second, 8) * first).astype(BF)
    tail = tail_of(ao * ag)
    for q in range(2):
        scratch[q, 0:256] = joined[256 * q : 256 * q + 256]
        scratch[q, 256:272] = tail
    keep_ref[...] = scratch[x]
    send_ref[...] = scratch[1 - x]


def k_chip(reverse, sc, own, got, out_ref):
    x = sc[5]
    mine_first = first_of(reverse, x)
    so, sg = own[0:256].astype(F32), got[0:256].astype(F32)
    ao, ag = decays_of(own[256:272]), decays_of(got[256:272])
    first, second = jnp.where(mine_first, so, sg), jnp.where(mine_first, sg, so)
    a_second = jnp.where(mine_first, ag, ao)
    out_ref[0:256] = (second + quarter_rows(a_second, x) * first).astype(BF)
    out_ref[256:272] = tail_of(ao * ag)


def k_two(sc, near, far, out_ref):
    x = sc[5]
    a = decays_of(near[256:272])
    out_ref[...] = (near[0:256].astype(F32) + quarter_rows(a, x) * far[0:256].astype(F32)).astype(BF)


def k_four(reverse, sc, near, far, pair, older, own, got, keep_ref, send_ref):
    x = sc[5]
    a = decays_of(near[256:272]) * decays_of(far[256:272])
    before = pair[...].astype(F32) + quarter_rows(a, x) * older[...].astype(F32)
    mine_first = first_of(reverse, x)
    first = jnp.where(mine_first, own[0:256].astype(F32), got[0:256].astype(F32))
    a_first = jnp.where(mine_first, decays_of(own[256:272]), decays_of(got[256:272]))
    after = first + quarter_rows(a_first, x) * before
    keep_ref[...] = jnp.where(mine_first, before, after).astype(BF)
    send_ref[...] = jnp.where(mine_first, after, before).astype(BF)


def k_slab(reverse, sc, mine, other, own, got, keep_ref, send_ref, scratch):
    core, x = sc[4], sc[5]
    scratch[x] = mine[...]
    scratch[1 - x] = other[...]
    before = jnp.concatenate([scratch[0], scratch[1]], axis=0).astype(F32)
    mine_first = first_of(reverse, core)
    first = jnp.where(mine_first, own[0:512].astype(F32), got[0:512].astype(F32))
    a_first = jnp.where(mine_first, decays_of(own[512:528]), decays_of(got[512:528]))
    after = first + per_row(a_first, 8) * before
    keep_ref[...] = jnp.where(mine_first, before, after).astype(BF)
    send_ref[...] = jnp.where(mine_first, after, before).astype(BF)


def along(distance, reverse):
    if reverse:
        return [(i, i - distance) for i in range(distance, 8)]
    return [(i, i + distance) for i in range(8 - distance)]


def scan(reverse, tag, sc, keep, send):
    swap = [(0, 1), (1, 0)]
    part = functools.partial
    half = sds((512, 128), BF)
    quarter, tailed = sds((256, 128), BF), sds((272, 128), BF)
    got = lax.ppermute(send, "c", swap)
    own_q, send_q = call_scratch(
        part(k_core, reverse), (tailed, tailed), "core" + tag, 1, (sc, keep, got), [pltpu.VMEM((2, 272, 128), BF)], 10**6
    )
    got_q = lax.ppermute(send_q, "xl", swap)
    plane = call(part(k_chip, reverse), tailed, "chip" + tag, 1, (sc, own_q, got_q), 10**6)
    near = lax.ppermute(plane, "z", along(1, reverse))
    far = lax.ppermute(plane, "z", along(2, reverse))
    two = call(k_two, quarter, "two" + tag, 1, (sc, near, far), 10**6)
    older = lax.ppermute(two, "z", along(2, reverse))
    keep_q, out_q = call(
        part(k_four, reverse), (quarter, quarter), "four" + tag, 1, (sc, near, far, two, older, own_q, got_q), 10**6
    )
    back_q = lax.ppermute(out_q, "xl", swap)
    keep_h, out_h = call_scratch(
        part(k_slab, reverse), (half, half), "slab" + tag, 1, (sc, keep_q, back_q, keep, got), [pltpu.VMEM((2, 256, 128), BF)], 10**6
    )
    back_h = lax.ppermute(out_h, "c", swap)
    return keep_h, back_h


def slab_out(reverse, tag, sc, skip, parts, b, c, values, state):
    cum, cum_t, dt_t, late = parts
    base = call_scratch(
        functools.partial(k_inside, reverse),
        sds((T, 1024), F32),
        "inside" + tag,
        2,
        (sc, skip, cum, cum_t, dt_t, b, c, values),
        [pltpu.VMEM((T, T), F32), pltpu.VMEM((T, T), F32)],
        10**9,
    )
    side = b if reverse else c
    return call_scratch(
        k_final,
        sds((T, 1024), BF),
        "final" + tag,
        1,
        (sc, base, late, side, state[0], state[1]),
        [pltpu.VMEM((2, 512, 128), BF)],
        10**7,
    )


def body(hidden, values, seg_next, proj_bc, proj_dt, dt_bias, decay, skip, bc_prev, dt_prev, seg_prev, grads):
    z, x, c = (lax.axis_index(n) for n in SEQ)
    k = lax.axis_index(FSDP)
    slab = lax.axis_index(SEQ)

    def scalars(lengths):
        b0 = lengths[0]
        b1 = b0 + lengths[1]
        b2 = b1 + lengths[2]
        return jnp.stack([b0, b1, b2, slab * T, c, x, z, k]).astype(jnp.int32)

    sc_next, sc_prev = scalars(seg_next), scalars(seg_prev)
    params = jnp.tile(lax.dynamic_slice_in_dim(jnp.stack([decay, dt_bias]), HEADS * k, HEADS, 1), (1, 8))

    weights = gather_weights(sc_next, proj_bc, proj_dt)

    group = k // 2
    b_prev = lax.dynamic_slice_in_dim(bc_prev, 128 * group, 128, 1)
    c_prev = lax.dynamic_slice_in_dim(bc_prev, 512 + 128 * group, 128, 1)
    dt_wide = jnp.tile(dt_prev, (1, 8))
    local = call_scratch(
        k_local_prev, LOCAL_OUTS, "local_prev", 1, (sc_prev, dt_wide, params, b_prev, c_prev, grads), [pltpu.VMEM((2, 528, 128), BF)], 10**8
    )
    state = scan(True, "_prev", sc_prev, local[0], local[1])
    grad_values = slab_out(True, "_prev", sc_prev, skip, local[2:6], b_prev, c_prev, grads, state)

    mine, dt_raw = call(k_project, (sds((T, 128), BF), sds((T, 128), F32)), "project", 1, (sc_next, hidden) + weights, 10**9)
    pair = lax.ppermute(mine, "y", [(i, i ^ 1) for i in range(4)])
    wide = sds((T, 128), BF)
    local = call_scratch(
        k_local_next, LOCAL_OUTS + (wide, wide), "local_next", 1, (sc_next, dt_raw, params, mine, pair, values), [pltpu.VMEM((2, 528, 128), BF)], 10**8
    )
    state = scan(False, "_next", sc_next, local[0], local[1])
    out_next = slab_out(False, "_next", sc_next, skip, local[2:6], local[6], local[7], values, state)
    return out_next, grad_values


def solution(mesh):
    split = Mesh(mesh.devices.reshape(8, 2, 2, 2, 4), ("z", "xl", "c", "xh", "y"))
    all_axes = SEQ + FSDP
    in_specs = (
        P(SEQ, None),
        P(SEQ, FSDP),
        P(),
        P(all_axes, None),
        P(all_axes, None),
        P(),
        P(),
        P(),
        P(SEQ, None),
        P(SEQ, FSDP),
        P(),
        P(SEQ, FSDP),
    )
    out_specs = (P(SEQ, FSDP), P(SEQ, FSDP))
    return jax.shard_map(body, mesh=split, in_specs=in_specs, out_specs=out_specs, check_vma=False)
```

time: 395 us -> 153 us (0.39)
  waiting for transfers between devices: 200 us -> 13 us
  blocking collectives: 111 us -> 14.5 us
  starting transfers between devices: 0.33 us -> 51.7 us
  Pallas kernels: 0 us -> 47.7 us
  other arithmetic: 30.4 us -> 0.68 us
  matrix products: 11.8 us -> 0 us
  between operations: 15 us -> 4.66 us
  local copies, waits for them, and re-layouts: 26.2 us -> 20 us
    all_gather x7 -> x0, waiting for transfers between devices: 187 us -> none  [the longest x6 132 us: prefix_by_axis(): pieces = jax.tree.map(lambda part: lax.all_gather(part, axis), so_far)]
    psum x1 -> x0, blocking collectives: 67.7 us -> none  [body(): lax.psum((jnp.dot(owned, pieces[0], preferred_element_type=jnp.float32),...]
    ppermute x0 -> x26, starting transfers between devices: none -> 51.7 us  [the longest x3 11.7 us: gather_weights(): now = lax.ppermute(now, ('z', 'c'), ring)]
    pallas_call x0 -> x20, Pallas kernels: none -> 47.7 us  [the longest x10 28 us: call_scratch(): pl.pallas_call(kernel, out_shape=outs, in_specs=[SM] * n_smem + [VM] * (l...]
    all_gather x6 -> x0, blocking collectives: 42.9 us -> none  [prefix_by_axis(): pieces = jax.tree.map(lambda part: lax.all_gather(part, axis), so_far)]
    all_to_all x0 -> x1, blocking collectives: none -> 14.5 us  [gather_weights(): got = lax.all_to_all(send, FSDP, 0, 0, tiled=False)]
    psum x1 -> x0, waiting for transfers between devices: 13.6 us -> none  [body(): lax.psum((jnp.dot(owned, pieces[0], preferred_element_type=jnp.float32),...]
    ppermute x0 -> x26, waiting for transfers between devices: none -> 13 us  [the longest x3 11.3 us: gather_weights(): now = lax.ppermute(now, ('z', 'c'), ring)]
  transfers between devices with their start and end apart: 8 -> 26, of which waited for: 7 -> 5; matrix products, arithmetic and copies ran while one was open for 13% -> 4% of each run, Pallas kernels for 0% -> 23%
where the time goes in v1:
time: 153 us; the launch traced here: 152 us
  starting transfers between devices  51.7 us (34%)
  Pallas kernels  47.7 us (31%)
  local copies, waits for them, and re-layouts  20 us (13%)
  blocking collectives  14.5 us (9%)
  waiting for transfers between devices  13 us (8%)
  between operations  4.66 us (3%)
    pallas_call x10, Pallas kernels, call_scratch(): pl.pallas_call(kernel, out_shape=outs, in_specs=[SM] * n_smem + [VM] * (l...  28 us
    pallas_call x10, Pallas kernels, call(): pl.pallas_call(kernel, out_shape=outs, in_specs=[SM] * n_smem + [VM] * (l...  19.7 us
    all_to_all x1, blocking collectives, gather_weights(): got = lax.all_to_all(send, FSDP, 0, 0, tiled=False)  14.5 us
    ppermute x3, starting transfers between devices, gather_weights(): now = lax.ppermute(now, ('z', 'c'), ring)  11.7 us
    unnamed x54, local copies, waits for them, and re-layouts  11.6 us
    ppermute x3, waiting for transfers between devices, gather_weights(): now = lax.ppermute(now, ('z', 'c'), ring)  11.3 us
    ppermute x2, starting transfers between devices, scan(): far = lax.ppermute(plane, 'z', along(2, reverse))  6.18 us
    ppermute x2, starting transfers between devices, scan(): older = lax.ppermute(two, 'z', along(2, reverse))  6.16 us
  transfers between devices with their start and end apart: 26, of which 5 were waited for; matrix products, arithmetic and copies ran while one was open for 4% of the time, Pallas kernels for 23%

profile of v1, /device:TPU:1, one launch (start us, length us, event | category | flops | bytes accessed | tf_op | source)
XLA Modules:
  0.0 152.3 jit_solution(2754484693622664225)
XLA Ops:
  6.8 14.5 %all_to_all.5.rec_ref = bf16[8,64,128]{2,1,0:T(8,128)(2,1)} all-to-all(bf16[8,64,128]{2,1,0:T(8,128)(2,1)} %columns.1), channel_id=1, replica_groups=mesh['z'=8,'xl'=2,'c'=2,'xh'=2,'y'=4] {'xh','y'}, dimensions={0} | all-to-all | bytes 262144 | tf_op jit(solution)/shard_map/all_to_all | solution.py:108
  23.2 2.4 %collective-permute-start.1 = (bf16[288,128]{1,0:T(8,128)(2,1)}, bf16[288,128]{1,0:T(8,128)(2,1)S(1)}, u32[]{:S(2)}, u32[]{:S(2)}) collective-permute-start(bf16[288,128]{1,0:T(8,128)(2,1)} %rows.1.own), channel_id=1, source_target_pairs={{0,8},{8,0},{1,9},{9,1},{2,10},{10,2},{3,11},{11,3},{4,12},{12,4},... | collective-permute-start | bytes 221192 | tf_op jit(solution)/shard_map/ppermute | solution.py:112
  26.3 3.3 %collective-permute-start.2 = (bf16[288,128]{1,0:T(8,128)(2,1)S(1)}, bf16[288,128]{1,0:T(8,128)(2,1)S(1)}, u32[]{:S(2)}, u32[]{:S(2)}) collective-permute-start(bf16[288,128]{1,0:T(8,128)(2,1)S(1)} %collective-permute-done.other_x), channel_id=1, source_target_pairs={{0,8},{8,0},{1,9},{9,1},{2,10},{10,2},{3,11},{11,3},{4,12},{12,4},... | collective-permute-start | bytes 221192 | tf_op jit(solution)/shard_map/ppermute | solution.py:113
  32.8 5.6 %collective-permute-start.3 = (bf16[4,288,128]{2,1,0:T(8,128)(2,1)}, bf16[4,288,128]{2,1,0:T(8,128)(2,1)S(1)}, u32[]{:S(2)}, u32[]{:S(2)}) collective-permute-start(bf16[4,288,128]{2,1,0:T(8,128)(2,1)} %quad.1.q0), channel_id=1, source_target_pairs={{0,32},{32,64},{64,96},{96,128},{128,160},{160,192},{192,224},{224... | collective-permute-start | bytes 884744 | tf_op jit(solution)/shard_map/ppermute | solution.py:118
  38.4 4.0 %collective-permute-done.3.r1 = bf16[4,288,128]{2,1,0:T(8,128)(2,1)S(1)} collective-permute-done((bf16[4,288,128]{2,1,0:T(8,128)(2,1)}, bf16[4,288,128]{2,1,0:T(8,128)(2,1)S(1)}, u32[]{:S(2)}, u32[]{:S(2)}) %collective-permute-start.3) | collective-permute-done | bytes 294944 | tf_op jit(solution)/shard_map/ppermute | solution.py:118
  42.4 3.0 %collective-permute-start.5 = (bf16[4,288,128]{2,1,0:T(8,128)(2,1)S(1)}, bf16[4,288,128]{2,1,0:T(8,128)(2,1)S(1)}, u32[]{:S(2)}, u32[]{:S(2)}) collective-permute-start(bf16[4,288,128]{2,1,0:T(8,128)(2,1)S(1)} %collective-permute-done.3.r1), channel_id=1, source_target_pairs={{0,32},{32,64},{64,96},{96,128},{128,160},{160,192},{192,224},{224... | collective-permute-start | bytes 884744 | tf_op jit(solution)/shard_map/ppermute | solution.py:118
  45.4 3.7 %collective-permute-done.5.r2 = bf16[4,288,128]{2,1,0:T(8,128)(2,1)S(1)} collective-permute-done((bf16[4,288,128]{2,1,0:T(8,128)(2,1)S(1)}, bf16[4,288,128]{2,1,0:T(8,128)(2,1)S(1)}, u32[]{:S(2)}, u32[]{:S(2)}) %collective-permute-start.5) | collective-permute-done | bytes 294944 | tf_op jit(solution)/shard_map/ppermute | solution.py:118
  49.1 3.1 %collective-permute-start.7 = (bf16[4,288,128]{2,1,0:T(8,128)(2,1)S(1)}, bf16[4,288,128]{2,1,0:T(8,128)(2,1)S(1)}, u32[]{:S(2)}, u32[]{:S(2)}) collective-permute-start(bf16[4,288,128]{2,1,0:T(8,128)(2,1)S(1)} %collective-permute-done.5.r2), channel_id=1, source_target_pairs={{0,32},{32,64},{64,96},{96,128},{128,160},{160,192},{192,224},{224... | collective-permute-start | bytes 884744 | tf_op jit(solution)/shard_map/ppermute | solution.py:118
  52.2 3.7 %collective-permute-done.7.r3 = bf16[4,288,128]{2,1,0:T(8,128)(2,1)S(1)} collective-permute-done((bf16[4,288,128]{2,1,0:T(8,128)(2,1)S(1)}, bf16[4,288,128]{2,1,0:T(8,128)(2,1)S(1)}, u32[]{:S(2)}, u32[]{:S(2)}) %collective-permute-start.7) | collective-permute-done | bytes 294944 | tf_op jit(solution)/shard_map/ppermute | solution.py:118
  55.9 3.2 %collective-permute-start.9 = (bf16[2,288,128]{2,1,0:T(8,128)(2,1)S(1)}, bf16[2,288,128]{2,1,0:T(8,128)(2,1)S(1)}, u32[]{:S(2)}, u32[]{:S(2)}) collective-permute-start(bf16[2,288,128]{2,1,0:T(8,128)(2,1)S(1)} %constant_dynamic-slice_fusion.3), channel_id=1, source_target_pairs={{0,32},{32,64},{64,96},{96,128},{128,160},{160,192},{192,224},{224... | collective-permute-start | bytes 442376 | tf_op jit(solution)/shard_map/ppermute | solution.py:122
  61.9 4.4 %collective-permute-start.10 = (bf16[2,288,128]{2,1,0:T(8,128)(2,1)S(1)}, bf16[2,288,128]{2,1,0:T(8,128)(2,1)S(1)}, u32[]{:S(2)}, u32[]{:S(2)}) collective-permute-start(bf16[2,288,128]{2,1,0:T(8,128)(2,1)S(1)} %collective-permute-done.9.h_own), channel_id=1, source_target_pairs={{0,8},{8,0},{1,9},{9,1},{2,10},{10,2},{3,11},{11,3},{4,12},{12,4},... | collective-permute-start | bytes 442376 | tf_op jit(solution)/shard_map/ppermute | solution.py:123
  70.1 4.9 %project.1 = (bf16[256,128]{1,0:T(8,128)(2,1)}, f32[256,128]{1,0:T(8,128)}) custom-call(s32[8]{0:T(128)} %stack.44.sc, bf16[256,8192]{1,0:T(8,128)(2,1)} %hid.1, bf16[4,288,128]{2,1,0:T(8,128)(2,1)} %quad.1.q0, bf16[4,288,128]{2,1,0:T(8,128)(2,1)} %copy-done.3, bf16[4,288,128]{2,1,0:T(8,128)(2,1)} %copy-done.5, bf16[4,288,128]{2,1,0:T(8,128)(2,1)} %copy-done.4, ...), custom_call_target="tpu_custom_call" | custom-call | flops 1000000000 | bytes 1000000 | tf_op jit(solution)/shard_map/project/pallas_call | solution.py:23
  80.0 3.8 %local_prev.1 = (bf16[528,128]{1,0:T(8,128)(2,1)}, bf16[528,128]{1,0:T(8,128)(2,1)}, f32[256,128]{1,0:T(8,128)}, f32[16,256]{1,0:T(8,128)}, f32[16,256]{1,0:T(8,128)}, /*index=5*/f32[256,128]{1,0:T(8,128)}) custom-call(s32[8]{0:T(128)} %stack.48.sc, f32[256,128]{1,0:T(8,128)} %copy.15.dt_ref, f32[2,128]{1,0:T(2,128)} %tile.9.par, ...), custom_call_target="tpu_custom_call" | custom-call | flops 100000000 | bytes 2000000 | tf_op jit(solution)/shard_map/local_prev/pallas_call | solution.py:216
  84.8 3.8 %local_next.1 = (bf16[528,128]{1,0:T(8,128)(2,1)}, bf16[528,128]{1,0:T(8,128)(2,1)}, f32[256,128]{1,0:T(8,128)}, f32[16,256]{1,0:T(8,128)}, f32[16,256]{1,0:T(8,...) custom-call(s32[8]{0:T(128)} %stack.44.sc, f32[256,128]{1,0:T(8,128)} %get-tuple-element.30.dt_ref, ...), custom_call_target="tpu_custom_call" | custom-call | flops 100000000 | bytes 2000000 | tf_op jit(solution)/shard_map/local_next/pallas_call | solution.py:216
  102.2 4.0 %collective-permute-start.14 = (bf16[272,128]{1,0:T(8,128)(2,1)}, bf16[272,128]{1,0:T(8,128)(2,1)S(1)}, u32[]{:S(2)}, u32[]{:S(2)}) collective-permute-start(bf16[272,128]{1,0:T(8,128)(2,1)} %chip_next.1), channel_id=1, source_target_pairs={{0,32},{32,64},{64,96},{96,128},{128,160},{160,192},{192,224},{1,3... | collective-permute-start | bytes 208904 | tf_op jit(solution)/shard_map/ppermute | solution.py:372
  106.1 4.9 %collective-permute-start.15 = (bf16[272,128]{1,0:T(8,128)(2,1)}, bf16[272,128]{1,0:T(8,128)(2,1)S(1)}, u32[]{:S(2)}, u32[]{:S(2)}) collective-permute-start(bf16[272,128]{1,0:T(8,128)(2,1)} %chip_next.1), channel_id=1, source_target_pairs={{0,64},{32,96},{64,128},{96,160},{128,192},{160,224},{1,65},{33,97... | collective-permute-start | bytes 208904 | tf_op jit(solution)/shard_map/ppermute | solution.py:373
  118.0 4.9 %collective-permute-start.16 = (bf16[256,128]{1,0:T(8,128)(2,1)}, bf16[256,128]{1,0:T(8,128)(2,1)S(1)}, u32[]{:S(2)}, u32[]{:S(2)}) collective-permute-start(bf16[256,128]{1,0:T(8,128)(2,1)} %two_next.1.pair), channel_id=1, source_target_pairs={{0,64},{32,96},{64,128},{96,160},{128,192},{160,224},{1,65},{33,97... | collective-permute-start | bytes 196616 | tf_op jit(solution)/shard_map/ppermute | solution.py:375
  129.8 1.9 %slab_prev.1 = (bf16[512,128]{1,0:T(8,128)(2,1)}, bf16[512,128]{1,0:T(8,128)(2,1)}) custom-call(s32[8]{0:T(128)} %stack.48.sc, bf16[256,128]{1,0:T(8,128)(2,1)} %get-tuple-element.54.mine, bf16[256,128]{1,0:T(8,128)(2,1)} %copy-done.22, bf16[528,128]{1,0:T(8,128)(2,1)} %get-tuple-element.50.own, bf16[528,128]{1,0:T(8,128)(2,1)} %copy-done.1), custom_call_target="tpu_custom_call" | custom-call | flops 1000000 | bytes 2000000 | tf_op jit(solution)/shard_map/slab_prev/pallas_call | solution.py:216
  131.7 3.6 %collective-permute-start.25 = (bf16[512,128]{1,0:T(8,128)(2,1)}, bf16[512,128]{1,0:T(8,128)(2,1)S(1)}, u32[]{:S(2)}, u32[]{:S(2)}) collective-permute-start(bf16[512,128]{1,0:T(8,128)(2,1)} %get-tuple-element.57), channel_id=1, source_target_pairs={{0,8},{8,0},{1,9},{9,1},{2,10},{10,2},{3,11},{11,3},{4,12},{12,4},... | collective-permute-start | bytes 393224 | tf_op jit(solution)/shard_map/ppermute | solution.py:383
  135.9 1.9 %slab_next.1 = (bf16[512,128]{1,0:T(8,128)(2,1)}, bf16[512,128]{1,0:T(8,128)(2,1)}) custom-call(s32[8]{0:T(128)} %stack.44.sc, bf16[256,128]{1,0:T(8,128)(2,1)} %get-tuple-element.42.mine, bf16[256,128]{1,0:T(8,128)(2,1)} %copy-done.23, bf16[528,128]{1,0:T(8,128)(2,1)} %get-tuple-element.38.own, bf16[528,128]{1,0:T(8,128)(2,1)} %copy-done.2), custom_call_target="tpu_custom_call" | custom-call | flops 1000000 | bytes 2000000 | tf_op jit(solution)/shard_map/slab_next/pallas_call | solution.py:216
  137.9 3.7 %inside_prev.1.base_ref = f32[256,1024]{1,0:T(8,128)} custom-call(s32[8]{0:T(128)} %stack.48.sc, f32[128]{0:T(128)} %skip.3, f32[256,128]{1,0:T(8,128)} %get-tuple-element.46.cum_ref, f32[16,256]{1,0:T(8,128)} %get-tuple-element.47.cumt_ref, f32[16,256]{1,0:T(8,128)} %get-tuple-element.48.dtt_ref, bf16[256,128]{1,0:T(8,128)(2,1)} %get-tuple-element.59.b_ref.side_ref, ...), custom_call_target="tpu_custom_call" | custom-call | flops 1000000000 | bytes 2000000 | tf_op jit(solution)/shard_map/inside_prev/pallas_call | solution.py:216
  142.3 2.9 %final_prev.1 = bf16[256,1024]{1,0:T(8,128)(2,1)} custom-call(s32[8]{0:T(128)} %stack.48.sc, f32[256,1024]{1,0:T(8,128)} %inside_prev.1.base_ref, f32[256,128]{1,0:T(8,128)} %get-tuple-element.49.late_ref, bf16[256,128]{1,0:T(8,128)(2,1)} %get-tuple-element.59.b_ref.side_ref, bf16[512,128]{1,0:T(8,128)(2,1)} %get-tuple-element.56.keep_ref, ...), custom_call_target="tpu_custom_call" | custom-call | flops 10000000 | bytes 2000000 | tf_op jit(solution)/shard_map/final_prev/pallas_call | solution.py:216
  145.1 3.7 %inside_next.1.base_ref = f32[256,1024]{1,0:T(8,128)} custom-call(s32[8]{0:T(128)} %stack.44.sc, f32[128]{0:T(128)} %skip.3, f32[256,128]{1,0:T(8,128)} %get-tuple-element.32.cum_ref, f32[16,256]{1,0:T(8,128)} %get-tuple-element.33.cumt_ref, f32[16,256]{1,0:T(8,128)} %get-tuple-element.34.dtt_ref, bf16[256,128]{1,0:T(8,128)(2,1)} %get-tuple-element.35.b_ref, ...), custom_call_target="tpu_custom_call" | custom-call | flops 1000000000 | bytes 2000000 | tf_op jit(solution)/shard_map/inside_next/pallas_call | solution.py:216
  149.4 2.9 %final_next.1 = bf16[256,1024]{1,0:T(8,128)(2,1)} custom-call(s32[8]{0:T(128)} %stack.44.sc, f32[256,1024]{1,0:T(8,128)} %inside_next.1.base_ref, f32[256,128]{1,0:T(8,128)} %get-tuple-element.37.late_ref, bf16[256,128]{1,0:T(8,128)(2,1)} %get-tuple-element.36.c_ref.side_ref, bf16[512,128]{1,0:T(8,128)(2,1)} %get-tuple-element.44.keep_ref, ...), custom_call_target="tpu_custom_call" | custom-call | flops 10000000 | bytes 2000000 | tf_op jit(solution)/shard_map/final_next/pallas_call | solution.py:216
  (115 shorter events, 50.2 us)
Async XLA Ops:
  23.2 6.4 %collective-permute-start.1 = (bf16[288,128]{1,0:T(8,128)(2,1)}, bf16[288,128]{1,0:T(8,128)(2,1)S(1)}, u32[]{:S(2)}, u32[]{:S(2)}) collective-permute-start(bf16[288,128]{1,0:T(8,128)(2,1)} %rows.1.own), channel_id=1, source_target_pairs={{0,8},{8,0},{1,9},{9,1},{2,10},{10,2},{3,11},{11,3},{4,12},{12,4},... | collective-permute-start | bytes 221192 | tf_op jit(solution)/shard_map/ppermute | solution.py:112
  26.3 4.2 %collective-permute-start.2 = (bf16[288,128]{1,0:T(8,128)(2,1)S(1)}, bf16[288,128]{1,0:T(8,128)(2,1)S(1)}, u32[]{:S(2)}, u32[]{:S(2)}) collective-permute-start(bf16[288,128]{1,0:T(8,128)(2,1)S(1)} %collective-permute-done.other_x), channel_id=1, source_target_pairs={{0,8},{8,0},{1,9},{9,1},{2,10},{10,2},{3,11},{11,3},{4,12},{12,4},... | collective-permute-start | bytes 221192 | tf_op jit(solution)/shard_map/ppermute | solution.py:113
  32.8 9.6 %collective-permute-start.3 = (bf16[4,288,128]{2,1,0:T(8,128)(2,1)}, bf16[4,288,128]{2,1,0:T(8,128)(2,1)S(1)}, u32[]{:S(2)}, u32[]{:S(2)}) collective-permute-start(bf16[4,288,128]{2,1,0:T(8,128)(2,1)} %quad.1.q0), channel_id=1, source_target_pairs={{0,32},{32,64},{64,96},{96,128},{128,160},{160,192},{192,224},{224... | collective-permute-start | bytes 884744 | tf_op jit(solution)/shard_map/ppermute | solution.py:118
  42.4 6.7 %collective-permute-start.5 = (bf16[4,288,128]{2,1,0:T(8,128)(2,1)S(1)}, bf16[4,288,128]{2,1,0:T(8,128)(2,1)S(1)}, u32[]{:S(2)}, u32[]{:S(2)}) collective-permute-start(bf16[4,288,128]{2,1,0:T(8,128)(2,1)S(1)} %collective-permute-done.3.r1), channel_id=1, source_target_pairs={{0,32},{32,64},{64,96},{96,128},{128,160},{160,192},{192,224},{224... | collective-permute-start | bytes 884744 | tf_op jit(solution)/shard_map/ppermute | solution.py:118
  49.1 6.8 %collective-permute-start.7 = (bf16[4,288,128]{2,1,0:T(8,128)(2,1)S(1)}, bf16[4,288,128]{2,1,0:T(8,128)(2,1)S(1)}, u32[]{:S(2)}, u32[]{:S(2)}) collective-permute-start(bf16[4,288,128]{2,1,0:T(8,128)(2,1)S(1)} %collective-permute-done.5.r2), channel_id=1, source_target_pairs={{0,32},{32,64},{64,96},{96,128},{128,160},{160,192},{192,224},{224... | collective-permute-start | bytes 884744 | tf_op jit(solution)/shard_map/ppermute | solution.py:118
  55.9 6.0 %collective-permute-start.9 = (bf16[2,288,128]{2,1,0:T(8,128)(2,1)S(1)}, bf16[2,288,128]{2,1,0:T(8,128)(2,1)S(1)}, u32[]{:S(2)}, u32[]{:S(2)}) collective-permute-start(bf16[2,288,128]{2,1,0:T(8,128)(2,1)S(1)} %constant_dynamic-slice_fusion.3), channel_id=1, source_target_pairs={{0,32},{32,64},{64,96},{96,128},{128,160},{160,192},{192,224},{224... | collective-permute-start | bytes 442376 | tf_op jit(solution)/shard_map/ppermute | solution.py:122
  59.1 9.4 %collective-permute-start.4 = (bf16[4,288,128]{2,1,0:T(8,128)(2,1)S(1)}, bf16[4,288,128]{2,1,0:T(8,128)(2,1)S(1)}, u32[]{:S(2)}, u32[]{:S(2)}) collective-permute-start(bf16[4,288,128]{2,1,0:T(8,128)(2,1)S(1)} %collective-permute-done.3.r1), channel_id=1, source_target_pairs={{0,8},{8,0},{1,9},{9,1},{2,10},{10,2},{3,11},{11,3},{4,12},{12,4},... | collective-permute-start | bytes 884744 | tf_op jit(solution)/shard_map/ppermute | solution.py:120
  60.0 8.5 %collective-permute-start.6 = (bf16[4,288,128]{2,1,0:T(8,128)(2,1)S(1)}, bf16[4,288,128]{2,1,0:T(8,128)(2,1)S(1)}, u32[]{:S(2)}, u32[]{:S(2)}) collective-permute-start(bf16[4,288,128]{2,1,0:T(8,128)(2,1)S(1)} %collective-permute-done.5.r2), channel_id=1, source_target_pairs={{0,8},{8,0},{1,9},{9,1},{2,10},{10,2},{3,11},{11,3},{4,12},{12,4},... | collective-permute-start | bytes 884744 | tf_op jit(solution)/shard_map/ppermute | solution.py:120
  60.1 8.4 %collective-permute-start.8 = (bf16[4,288,128]{2,1,0:T(8,128)(2,1)S(1)}, bf16[4,288,128]{2,1,0:T(8,128)(2,1)S(1)}, u32[]{:S(2)}, u32[]{:S(2)}) collective-permute-start(bf16[4,288,128]{2,1,0:T(8,128)(2,1)S(1)} %collective-permute-done.7.r3), channel_id=1, source_target_pairs={{0,8},{8,0},{1,9},{9,1},{2,10},{10,2},{3,11},{11,3},{4,12},{12,4},... | collective-permute-start | bytes 884744 | tf_op jit(solution)/shard_map/ppermute | solution.py:120
  61.9 6.6 %collective-permute-start.10 = (bf16[2,288,128]{2,1,0:T(8,128)(2,1)S(1)}, bf16[2,288,128]{2,1,0:T(8,128)(2,1)S(1)}, u32[]{:S(2)}, u32[]{:S(2)}) collective-permute-start(bf16[2,288,128]{2,1,0:T(8,128)(2,1)S(1)} %collective-permute-done.9.h_own), channel_id=1, source_target_pairs={{0,8},{8,0},{1,9},{9,1},{2,10},{10,2},{3,11},{11,3},{4,12},{12,4},... | collective-permute-start | bytes 442376 | tf_op jit(solution)/shard_map/ppermute | solution.py:123
  75.0 9.2 %collective-permute-start.11 = (bf16[256,128]{1,0:T(8,128)(2,1)}, bf16[256,128]{1,0:T(8,128)(2,1)S(1)}, u32[]{:S(2)}, u32[]{:S(2)}) collective-permute-start(bf16[256,128]{1,0:T(8,128)(2,1)} %get-tuple-element.31.mine_ref), channel_id=1, source_target_pairs={{0,1},{1,0},{2,3},{3,2},{4,5},{5,4},{6,7},{7,6},{8,9},{9,8},{10,11... | collective-permute-start | bytes 196616 | tf_op jit(solution)/shard_map/ppermute | solution.py:437
  83.8 5.0 %collective-permute-start.19 = (bf16[528,128]{1,0:T(8,128)(2,1)}, bf16[528,128]{1,0:T(8,128)(2,1)S(1)}, u32[]{:S(2)}, u32[]{:S(2)}) collective-permute-start(bf16[528,128]{1,0:T(8,128)(2,1)} %get-tuple-element.51), channel_id=1, source_target_pairs={{0,8},{8,0},{1,9},{9,1},{2,10},{10,2},{3,11},{11,3},{4,12},{12,4},... | collective-permute-start | bytes 405512 | tf_op jit(solution)/shard_map/ppermute | solution.py:366
  91.2 3.9 %collective-permute-start.20 = (bf16[272,128]{1,0:T(8,128)(2,1)}, bf16[272,128]{1,0:T(8,128)(2,1)S(1)}, u32[]{:S(2)}, u32[]{:S(2)}) collective-permute-start(bf16[272,128]{1,0:T(8,128)(2,1)} %get-tuple-element.53), channel_id=1, source_target_pairs={{0,16},{16,0},{1,17},{17,1},{2,18},{18,2},{3,19},{19,3},{4,20},{20... | collective-permute-start | bytes 208904 | tf_op jit(solution)/shard_map/ppermute | solution.py:370
  94.0 6.0 %collective-permute-start.13 = (bf16[272,128]{1,0:T(8,128)(2,1)}, bf16[272,128]{1,0:T(8,128)(2,1)S(1)}, u32[]{:S(2)}, u32[]{:S(2)}) collective-permute-start(bf16[272,128]{1,0:T(8,128)(2,1)} %get-tuple-element.41), channel_id=1, source_target_pairs={{0,16},{16,0},{1,17},{17,1},{2,18},{18,2},{3,19},{19,3},{4,20},{20... | collective-permute-start | bytes 208904 | tf_op jit(solution)/shard_map/ppermute | solution.py:370
  97.4 13.7 %collective-permute-start.21 = (bf16[272,128]{1,0:T(8,128)(2,1)}, bf16[272,128]{1,0:T(8,128)(2,1)S(1)}, u32[]{:S(2)}, u32[]{:S(2)}) collective-permute-start(bf16[272,128]{1,0:T(8,128)(2,1)} %chip_prev.1), channel_id=1, source_target_pairs={{32,0},{64,32},{96,64},{128,96},{160,128},{192,160},{224,192},{33,... | collective-permute-start | bytes 208904 | tf_op jit(solution)/shard_map/ppermute | solution.py:372
  98.6 12.4 %collective-permute-start.22 = (bf16[272,128]{1,0:T(8,128)(2,1)}, bf16[272,128]{1,0:T(8,128)(2,1)S(1)}, u32[]{:S(2)}, u32[]{:S(2)}) collective-permute-start(bf16[272,128]{1,0:T(8,128)(2,1)} %chip_prev.1), channel_id=1, source_target_pairs={{64,0},{96,32},{128,64},{160,96},{192,128},{224,160},{65,1},{97,33... | collective-permute-start | bytes 208904 | tf_op jit(solution)/shard_map/ppermute | solution.py:373
  102.2 13.0 %collective-permute-start.14 = (bf16[272,128]{1,0:T(8,128)(2,1)}, bf16[272,128]{1,0:T(8,128)(2,1)S(1)}, u32[]{:S(2)}, u32[]{:S(2)}) collective-permute-start(bf16[272,128]{1,0:T(8,128)(2,1)} %chip_next.1), channel_id=1, source_target_pairs={{0,32},{32,64},{64,96},{96,128},{128,160},{160,192},{192,224},{1,3... | collective-permute-start | bytes 208904 | tf_op jit(solution)/shard_map/ppermute | solution.py:372
  106.1 9.0 %collective-permute-start.15 = (bf16[272,128]{1,0:T(8,128)(2,1)}, bf16[272,128]{1,0:T(8,128)(2,1)S(1)}, u32[]{:S(2)}, u32[]{:S(2)}) collective-permute-start(bf16[272,128]{1,0:T(8,128)(2,1)} %chip_next.1), channel_id=1, source_target_pairs={{0,64},{32,96},{64,128},{96,160},{128,192},{160,224},{1,65},{33,97... | collective-permute-start | bytes 208904 | tf_op jit(solution)/shard_map/ppermute | solution.py:373
  113.9 9.0 %collective-permute-start.23 = (bf16[256,128]{1,0:T(8,128)(2,1)}, bf16[256,128]{1,0:T(8,128)(2,1)S(1)}, u32[]{:S(2)}, u32[]{:S(2)}) collective-permute-start(bf16[256,128]{1,0:T(8,128)(2,1)} %two_prev.1.pair), channel_id=1, source_target_pairs={{64,0},{96,32},{128,64},{160,96},{192,128},{224,160},{65,1},{97,33... | collective-permute-start | bytes 196616 | tf_op jit(solution)/shard_map/ppermute | solution.py:375
  118.0 7.6 %collective-permute-start.16 = (bf16[256,128]{1,0:T(8,128)(2,1)}, bf16[256,128]{1,0:T(8,128)(2,1)S(1)}, u32[]{:S(2)}, u32[]{:S(2)}) collective-permute-start(bf16[256,128]{1,0:T(8,128)(2,1)} %two_next.1.pair), channel_id=1, source_target_pairs={{0,64},{32,96},{64,128},{96,160},{128,192},{160,224},{1,65},{33,97... | collective-permute-start | bytes 196616 | tf_op jit(solution)/shard_map/ppermute | solution.py:375
  125.3 3.9 %collective-permute-start.24 = (bf16[256,128]{1,0:T(8,128)(2,1)}, bf16[256,128]{1,0:T(8,128)(2,1)S(1)}, u32[]{:S(2)}, u32[]{:S(2)}) collective-permute-start(bf16[256,128]{1,0:T(8,128)(2,1)} %get-tuple-element.55), channel_id=1, source_target_pairs={{0,16},{16,0},{1,17},{17,1},{2,18},{18,2},{3,19},{19,3},{4,20},{20... | collective-permute-start | bytes 196616 | tf_op jit(solution)/shard_map/ppermute | solution.py:379
  128.0 7.2 %collective-permute-start.17 = (bf16[256,128]{1,0:T(8,128)(2,1)}, bf16[256,128]{1,0:T(8,128)(2,1)S(1)}, u32[]{:S(2)}, u32[]{:S(2)}) collective-permute-start(bf16[256,128]{1,0:T(8,128)(2,1)} %get-tuple-element.43), channel_id=1, source_target_pairs={{0,16},{16,0},{1,17},{17,1},{2,18},{18,2},{3,19},{19,3},{4,20},{20... | collective-permute-start | bytes 196616 | tf_op jit(solution)/shard_map/ppermute | solution.py:379
  131.7 9.9 %collective-permute-start.25 = (bf16[512,128]{1,0:T(8,128)(2,1)}, bf16[512,128]{1,0:T(8,128)(2,1)S(1)}, u32[]{:S(2)}, u32[]{:S(2)}) collective-permute-start(bf16[512,128]{1,0:T(8,128)(2,1)} %get-tuple-element.57), channel_id=1, source_target_pairs={{0,8},{8,0},{1,9},{9,1},{2,10},{10,2},{3,11},{11,3},{4,12},{12,4},... | collective-permute-start | bytes 393224 | tf_op jit(solution)/shard_map/ppermute | solution.py:383
  137.7 11.0 %collective-permute-start.18 = (bf16[512,128]{1,0:T(8,128)(2,1)}, bf16[512,128]{1,0:T(8,128)(2,1)S(1)}, u32[]{:S(2)}, u32[]{:S(2)}) collective-permute-start(bf16[512,128]{1,0:T(8,128)(2,1)} %get-tuple-element.45), channel_id=1, source_target_pairs={{0,8},{8,0},{1,9},{9,1},{2,10},{10,2},{3,11},{11,3},{4,12},{12,4},... | collective-permute-start | bytes 393224 | tf_op jit(solution)/shard_map/ppermute | solution.py:383
  (29 other events, 163.7 us)

commit v2 on v1

v2 whole, which is shorter than its diff:
```python
import functools
import jax
import jax.numpy as jnp
from jax import lax
from jax.experimental import pallas as pl
from jax.experimental.pallas import tpu as pltpu
from jax.sharding import Mesh
from jax.sharding import PartitionSpec as P

SEQ = ("z", "xl", "c")
FSDP = ("xh", "y")
BF = jnp.bfloat16
F32 = jnp.float32
T = 256
HEADS = 16
PAIRS = HEADS // 2
NEG = -1e30
VM = pl.BlockSpec(memory_space=pltpu.VMEM)
SM = pl.BlockSpec(memory_space=pltpu.SMEM)


def call(kernel, outs, name, n_smem, args, scratch=(), us=1, limit=12):
    return pl.pallas_call(
        kernel,
        out_shape=outs,
        in_specs=[SM] * n_smem + [VM] * (len(args) - n_smem),
        out_specs=jax.tree.map(lambda _: VM, outs),
        scratch_shapes=scratch,
        name=name,
        compiler_params=pltpu.CompilerParams(vmem_limit_bytes=limit << 20),
        cost_estimate=pl.CostEstimate(flops=us * 10_000_000, bytes_accessed=us * 100_000, transcendentals=0),
    )(*args)


def fsdp_place():
    return 4 * lax.axis_index("xh") + lax.axis_index("y")


def after(array, *others):
    return lax.optimization_barrier((array,) + others)[0]


def sds(shape, dtype):
    return jax.ShapeDtypeStruct(shape, dtype)


def lanes(shape):
    return lax.broadcasted_iota(jnp.int32, shape, len(shape) - 1)


def rows(shape):
    return lax.broadcasted_iota(jnp.int32, shape, len(shape) - 2)


def k_columns(bc_ref, dt_ref, out_ref):
    me = fsdp_place()
    lane = lanes((32, 128))
    low = lane < 64
    for j in range(4):
        b = bc_ref[:, 128 * j : 128 * j + 128].astype(F32)
        c = bc_ref[:, 512 + 128 * j : 640 + 128 * j].astype(F32)
        out_ref[2 * j, 0:32] = jnp.where(low, b, pltpu.roll(c, 64, 1)).astype(BF)
        out_ref[2 * j + 1, 0:32] = jnp.where(low, pltpu.roll(b, 64, 1), c).astype(BF)
    d = dt_ref[...].astype(F32)
    mine = lane // 16 == me
    for k in range(8):
        out_ref[k, 32:64] = jnp.where(mine, pltpu.roll(d, (16 * (me - k)) & 127, 1), 0.0).astype(BF)


def k_rows(rec_ref, out_ref):
    total = jnp.zeros((32, 128), F32)
    for k in range(8):
        out_ref[32 * k : 32 * k + 32] = rec_ref[k, 0:32]
        total = total + rec_ref[k, 32:64].astype(F32)
    out_ref[256:288] = total.astype(BF)


def k_quad(own, other_x, other_c, other_xc, out_ref):
    c, x = lax.axis_index("c"), lax.axis_index("xl")
    out_ref[2 * x + c] = own[...]
    out_ref[2 * (1 - x) + c] = other_x[...]
    out_ref[2 * x + 1 - c] = other_c[...]
    out_ref[2 * (1 - x) + 1 - c] = other_xc[...]


def weight_block(part):
    spread = (lanes((T, 128)) // 16) == (rows((T, 128)) // 32)
    packed = part[256:288]
    tall = jnp.concatenate([packed] * 8, axis=0)
    return jnp.concatenate([part[0:256], jnp.where(spread, tall, jnp.zeros_like(tall))], axis=1)


def times(hid, off, parts):
    left = hid[:, pl.ds(pl.multiple_of(off, 256), 256 * len(parts))]
    right = jnp.concatenate([weight_block(p) for p in parts], axis=0)
    return jnp.dot(left, right, preferred_element_type=F32)


def k_project_early(hid, q0, r1, g1, r2, g2, acc_ref):
    z, sign = lax.axis_index("z"), 1 - 2 * lax.axis_index("c")
    acc = times(hid, 1024 * z, [q0[b] for b in range(4)])
    for r, (up, down) in enumerate(((r1, g1), (r2, g2)), 1):
        acc = acc + times(hid, 1024 * ((z - sign * r) & 7), [up[b] for b in range(4)])
        acc = acc + times(hid, 1024 * ((z + sign * r) & 7), [down[b] for b in range(4)])
    acc_ref[...] = acc


def k_project_late(hid, early, r3, g3, h_own, h_other, y_ref, dt_ref):
    c, z = lax.axis_index("c"), lax.axis_index("z")
    sign = 1 - 2 * c
    acc = early[...] + times(hid, 1024 * ((z - sign * 3) & 7), [r3[b] for b in range(4)])
    acc = acc + times(hid, 1024 * ((z + sign * 3) & 7), [g3[b] for b in range(4)])
    far = 1024 * ((z + 4) & 7)
    acc = acc + times(hid, far + 512 * c, [h_own[b] for b in range(2)])
    acc = acc + times(hid, far + 512 * (1 - c), [h_other[b] for b in range(2)])
    y_ref[...] = acc[:, 0:128].astype(BF)
    d = acc[:, 128:256]
    for shift in (16, 32, 64):
        d = d + pltpu.roll(d, shift, 1)
    dt_ref[...] = d


def slab_start():
    return T * (4 * lax.axis_index("z") + 2 * lax.axis_index("xl") + lax.axis_index("c"))


def bounds_of(lengths):
    b0 = lengths[0]
    b1 = b0 + lengths[1]
    return b0, b1, b1 + lengths[2]


def segment_of(lengths, places):
    one, none = jnp.int32(1), jnp.int32(0)
    return sum((jnp.where(places >= b, one, none) for b in bounds_of(lengths)), none)


def expand(factor, j, low):
    a = jnp.broadcast_to(factor[:, 2 * j : 2 * j + 1], (T, 128))
    b = jnp.broadcast_to(factor[:, 2 * j + 1 : 2 * j + 2], (T, 128))
    return jnp.where(low, a, b)


def head_lanes(row):
    r = pltpu.roll(jnp.broadcast_to(row, (8, 128)), (128 - HEADS * fsdp_place()) & 127, 1)
    r = jnp.where(lanes((8, 128)) < HEADS, r, 0.0)
    for shift in (16, 32, 64):
        r = r + pltpu.roll(r, shift, 1)
    return r[0:1]


def local_part(reverse, sc, dt, dt_t, decay_row, b, c, val_ref, outs, scratch):
    keep_ref, send_ref, cum_ref, cumt_ref, dtt_ref, late_ref = outs
    offset, core = slab_start(), lax.axis_index("c")
    decay = head_lanes(decay_row)
    before, last = segment_of(sc, offset - 1), segment_of(sc, offset + T - 1)
    x = -jnp.transpose(dt * decay)[0:HEADS]
    lane = lanes((HEADS, T))
    for shift in (1, 2, 4, 8, 16, 32, 64, 128):
        x = x + jnp.where(lane >= shift, pltpu.roll(x, shift, 1), 0.0)
    cum_t = x
    cum = jnp.transpose(jnp.concatenate([cum_t] * 8, axis=0))
    final = cum[T - 1 : T]
    place = offset + rows((T, 128))
    seg = segment_of(sc, place)
    send = jnp.where(seg == last, jnp.exp(final - cum) * dt, 0.0)
    read = jnp.where(seg == before, jnp.exp(cum), 0.0)
    early, late = (read, send) if reverse else (send, read)
    cum_ref[...] = cum
    cumt_ref[...] = cum_t
    dtt_ref[...] = dt_t
    late_ref[...] = late
    low = lanes((T, 128)) < 64
    side = c if reverse else b
    for j in range(PAIRS):
        v = val_ref[:, 128 * j : 128 * j + 128].astype(F32)
        scaled = (v * expand(early, j, low)).astype(BF)
        out = lax.dot_general(scaled, side, (((0,), (0,)), ((), ())), preferred_element_type=F32)
        scratch[j // 4, 128 * (j % 4) : 128 * (j % 4) + 128] = out
    a = jnp.broadcast_to(jnp.exp(cum_t[:, T - 1 : T]), (HEADS, 128))
    a = jnp.where(last == before, a, 0.0)
    high = a.astype(BF).astype(F32)
    rest = a - high
    for half in range(2):
        pick = slice(8 * half, 8 * half + 8)
        scratch[half, 512:528] = jnp.concatenate([high[pick], rest[pick]], axis=0)
    keep_ref[...] = scratch[core]
    send_ref[...] = scratch[1 - core].astype(BF)


def group_columns(bc_ref, first):
    at = first + 128 * (fsdp_place() // 2)
    return bc_ref[:, pl.ds(pl.multiple_of(at, 128), 128)]


def k_local_prev(sc, dtt_ref, decay_ref, bc_ref, val_ref, *refs):
    dt_t = dtt_ref[...]
    dt = jnp.transpose(jnp.concatenate([dt_t] * 8, axis=0))
    local_part(True, sc, dt, dt_t, decay_ref[...], group_columns(bc_ref, 0), group_columns(bc_ref, 512), val_ref, refs[:6], refs[6])


def softplus(v):
    return jnp.maximum(v, 0.0) + jnp.log1p(jnp.exp(-jnp.abs(v)))


def k_local_next(sc, dt_ref, decay_ref, bias_ref, mine_ref, pair_ref, val_ref, *refs):
    outs, b_out, c_out, scratch = refs[:6], refs[6], refs[7], refs[8]
    odd = (lax.axis_index("y") & 1) == 1
    mine, pair = mine_ref[...].astype(F32), pair_ref[...].astype(F32)
    lo, hi = jnp.where(odd, pair, mine), jnp.where(odd, mine, pair)
    low = lanes((T, 128)) < 64
    b = jnp.where(low, lo, pltpu.roll(hi, 64, 1)).astype(BF)
    c = jnp.where(low, pltpu.roll(lo, 64, 1), hi).astype(BF)
    b_out[...] = b
    c_out[...] = c
    dt = softplus(dt_ref[...] + head_lanes(bias_ref[...]))
    local_part(False, sc, dt, jnp.transpose(dt)[0:HEADS], decay_ref[...], b, c, val_ref, outs, scratch)


LOCAL_OUTS = (
    sds((528, 128), F32),
    sds((528, 128), BF),
    sds((T, 128), F32),
    sds((HEADS, T), F32),
    sds((HEADS, T), F32),
    sds((T, 128), F32),
)


def sides(reverse, refs):
    if reverse:
        return group_columns(refs[0], 0), group_columns(refs[0], 512)
    return refs[0][...], refs[1][...]


def k_inside(reverse, sc, skip, cum_ref, cumt_ref, dtt_ref, val_ref, *refs):
    out_ref, bias_ref, score_ref = refs[-3:]
    offset, first_head = slab_start(), HEADS * fsdp_place()
    shape = (T, T)
    seg_r = segment_of(sc, offset + rows(shape))
    seg_l = segment_of(sc, offset + lanes(shape))
    causal = rows(shape) <= lanes(shape) if reverse else rows(shape) >= lanes(shape)
    bias_ref[...] = jnp.where((seg_r == seg_l) & causal, 0.0, NEG)
    b, c = sides(reverse, refs)
    one, two = (b, c) if reverse else (c, b)
    score_ref[...] = lax.dot_general(one, two, (((1,), (1,)), ((), ())), preferred_element_type=F32)
    low = lanes((T, 128)) < 64
    cum = cum_ref[...]
    for j in range(PAIRS):
        v = val_ref[:, 128 * j : 128 * j + 128]
        parts = []
        for h in (2 * j, 2 * j + 1):
            col = jnp.broadcast_to(cum[:, h : h + 1], shape)
            row = cumt_ref[h : h + 1]
            if reverse:
                spread = row - col
            else:
                spread = col - row
            decays = jnp.exp(spread + bias_ref[...])
            if reverse:
                mix = (decays * score_ref[...])
            else:
                mix = decays * dtt_ref[h : h + 1] * score_ref[...]
            parts.append(jnp.dot(mix.astype(BF), v, preferred_element_type=F32))
        inside = jnp.where(low, parts[0], parts[1])
        gain = jnp.where(low, skip[first_head + 2 * j], skip[first_head + 2 * j + 1])
        if reverse:
            dt = jnp.transpose(jnp.concatenate([dtt_ref[...]] * 8, axis=0)) if j == 0 else dt
            inside = inside * expand(dt, j, low)
        out_ref[:, 128 * j : 128 * j + 128] = inside + gain * v.astype(F32)


def k_final(reverse, base_ref, late_ref, keep_ref, got_ref, *refs):
    out_ref, scratch = refs[-2:]
    core = lax.axis_index("c")
    scratch[core] = keep_ref[...].astype(BF)
    scratch[1 - core] = got_ref[...]
    low = lanes((T, 128)) < 64
    late = late_ref[...]
    b, c = sides(reverse, refs)
    side = b if reverse else c
    for j in range(PAIRS):
        st = scratch[j // 4, 128 * (j % 4) : 128 * (j % 4) + 128]
        seen = lax.dot_general(side, st, (((1,), (1,)), ((), ())), preferred_element_type=F32)
        at = slice(128 * j, 128 * j + 128)
        out_ref[:, at] = (base_ref[:, at] + expand(late, j, low) * seen).astype(BF)


def decays_of(tail):
    t = tail.astype(F32)
    return t[0:8] + t[8:16]


def tail_of(a):
    high = a.astype(BF).astype(F32)
    return jnp.concatenate([high, a - high], axis=0)


def per_row(a, heads):
    return jnp.concatenate([jnp.broadcast_to(a[h : h + 1], (64, 128)) for h in range(heads)], axis=0)


def quarter_rows(a, which):
    return per_row(jnp.where(which == 0, a[0:4], a[4:8]), 4)


def first_of(reverse, bit):
    return (bit == 1) if reverse else (bit == 0)


def k_core(reverse, own, got, keep_ref, send_ref, scratch):
    core, x = lax.axis_index("c"), lax.axis_index("xl")
    mine_first = first_of(reverse, core)
    so, sg = own[0:512], got[0:512].astype(F32)
    ao, ag = decays_of(own[512:528]), decays_of(got[512:528])
    first, second = jnp.where(mine_first, so, sg), jnp.where(mine_first, sg, so)
    a_second = jnp.where(mine_first, ag, ao)
    joined = second + per_row(a_second, 8) * first
    tail = tail_of(ao * ag)
    for q in range(2):
        scratch[q, 0:256] = joined[256 * q : 256 * q + 256]
        scratch[q, 256:272] = tail
    keep_ref[...] = scratch[x]
    send_ref[...] = scratch[1 - x].astype(BF)


def k_chip(reverse, own, got, out_ref):
    x = lax.axis_index("xl")
    mine_first = first_of(reverse, x)
    so, sg = own[0:256], got[0:256].astype(F32)
    ao, ag = decays_of(own[256:272]), decays_of(got[256:272])
    first, second = jnp.where(mine_first, so, sg), jnp.where(mine_first, sg, so)
    a_second = jnp.where(mine_first, ag, ao)
    out_ref[0:256] = (second + quarter_rows(a_second, x) * first).astype(BF)
    out_ref[256:272] = tail_of(ao * ag).astype(BF)


def k_two(near, far, keep_ref, send_ref):
    x = lax.axis_index("xl")
    a = decays_of(near[256:272])
    two = near[0:256].astype(F32) + quarter_rows(a, x) * far[0:256].astype(F32)
    keep_ref[...] = two
    send_ref[...] = two.astype(BF)


def k_four(reverse, near, far, pair, older, own, got, keep_ref, send_ref):
    x = lax.axis_index("xl")
    a = decays_of(near[256:272]) * decays_of(far[256:272])
    before = pair[...] + quarter_rows(a, x) * older[...].astype(F32)
    mine_first = first_of(reverse, x)
    first = jnp.where(mine_first, own[0:256], got[0:256].astype(F32))
    a_first = jnp.where(mine_first, decays_of(own[256:272]), decays_of(got[256:272]))
    after = first + quarter_rows(a_first, x) * before
    keep_ref[...] = jnp.where(mine_first, before, after)
    send_ref[...] = jnp.where(mine_first, after, before).astype(BF)


def k_slab(reverse, mine, other, own, got, keep_ref, send_ref, scratch):
    core, x = lax.axis_index("c"), lax.axis_index("xl")
    scratch[x] = mine[...]
    scratch[1 - x] = other[...].astype(F32)
    before = jnp.concatenate([scratch[0], scratch[1]], axis=0)
    mine_first = first_of(reverse, core)
    first = jnp.where(mine_first, own[0:512], got[0:512].astype(F32))
    a_first = jnp.where(mine_first, decays_of(own[512:528]), decays_of(got[512:528]))
    after = first + per_row(a_first, 8) * before
    keep_ref[...] = jnp.where(mine_first, before, after)
    send_ref[...] = jnp.where(mine_first, after, before).astype(BF)


def along(distance, reverse):
    if reverse:
        return [(i, i - distance) for i in range(distance, 8)]
    return [(i, i + distance) for i in range(8 - distance)]


SWAP = [(0, 1), (1, 0)]
HALF, QUARTER, TAILED = (512, 128), (256, 128), (272, 128)


def both(shape):
    return sds(shape, F32), sds(shape, BF)


class Scan:
    def __init__(self, reverse, tag, keep, send):
        self.reverse, self.tag, self.keep, self.send = reverse, tag, keep, send

    def run(self, kernel, outs, name, args, scratch=()):
        return call(functools.partial(kernel, self.reverse), outs, name + self.tag, 0, args, scratch)

    def core(self):
        self.got = lax.ppermute(self.send, "c", SWAP)
        self.own_q, self.send_q = self.run(k_core, both(TAILED), "core", (self.keep, self.got), [pltpu.VMEM((2,) + TAILED, F32)])
        return self.send_q

    def chip(self):
        self.got_q = lax.ppermute(self.send_q, "xl", SWAP)
        self.plane = self.run(k_chip, sds(TAILED, BF), "chip", (self.own_q, self.got_q))
        return self.plane

    def two(self):
        self.near = lax.ppermute(self.plane, "z", along(1, self.reverse))
        self.far = lax.ppermute(self.plane, "z", along(2, self.reverse))
        self.pair, self.pair_send = call(k_two, both(QUARTER), "two" + self.tag, 0, (self.near, self.far))
        return self.pair_send

    def four(self):
        older = lax.ppermute(self.pair_send, "z", along(2, self.reverse))
        args = (self.near, self.far, self.pair, older, self.own_q, self.got_q)
        self.keep_q, self.out_q = self.run(k_four, both(QUARTER), "four", args)
        return self.out_q

    def slab(self):
        back = lax.ppermute(self.out_q, "xl", SWAP)
        args = (self.keep_q, back, self.keep, self.got)
        self.keep_h, self.out_h = self.run(k_slab, both(HALF), "slab", args, [pltpu.VMEM((2,) + QUARTER, F32)])
        return self.out_h

    def state(self):
        return self.keep_h, lax.ppermute(self.out_h, "c", SWAP)


def inside(reverse, tag, lengths, skip, parts, values, bc):
    cum, cum_t, dt_t, _ = parts
    args = (lengths, skip, cum, cum_t, dt_t, values) + bc
    scratch = [pltpu.VMEM((T, T), F32), pltpu.VMEM((T, T), F32)]
    return call(functools.partial(k_inside, reverse), sds((T, 1024), F32), "inside" + tag, 2, args, scratch, us=3)


def final(reverse, tag, base, late, state, bc):
    args = (base, late) + tuple(state) + bc
    kernel = functools.partial(k_final, reverse)
    return call(kernel, sds((T, 1024), BF), "final" + tag, 0, args, [pltpu.VMEM((2, 512, 128), BF)], us=2)


def body(hidden, values, seg_next, proj_bc, proj_dt, dt_bias, decay, skip, bc_prev, dt_prev, seg_prev, grads):
    decay_row, bias_row = decay[None, :], dt_bias[None, :]
    wide = sds((T, 128), BF)

    send = call(k_columns, sds((8, 64, 128), BF), "columns", 0, (proj_bc, proj_dt))
    got = lax.all_to_all(send, FSDP, 0, 0, tiled=False)
    own = call(k_rows, sds((288, 128), BF), "rows", 0, (got,))

    other_x = lax.ppermute(own, "xl", SWAP)
    other_c = lax.ppermute(own, "c", SWAP)
    other_xc = lax.ppermute(other_x, "c", SWAP)
    args = (after(seg_prev, own), dt_prev.T, decay_row, bc_prev, grads)
    local = call(k_local_prev, LOCAL_OUTS, "local_prev", 1, args, [pltpu.VMEM((2, 528, 128), F32)], us=3)
    prev = Scan(True, "_prev", local[0], local[1])
    parts_prev = local[2:6]
    q0 = call(k_quad, sds((4, 288, 128), BF), "quad", 0, (own, other_x, other_c, after(other_xc, local[1])))

    ring = [(2 * z, 2 * ((z + 1) % 8)) for z in range(8)] + [(2 * z + 1, 2 * ((z - 1) % 8) + 1) for z in range(8)]
    r1 = lax.ppermute(q0, ("z", "c"), ring)
    step = prev.core()
    r1 = after(r1, step)
    r2 = lax.ppermute(r1, ("z", "c"), ring)
    g1 = lax.ppermute(r1, "c", SWAP)
    step = prev.chip()
    r2 = after(r2, step, g1)
    r3 = lax.ppermute(r2, ("z", "c"), ring)
    g2 = lax.ppermute(r2, "c", SWAP)
    early = call(k_project_early, sds((T, 256), F32), "project_early", 0, (hidden, q0, r1, g1, r2, g2), us=3, limit=20)
    r3 = after(r3, early)
    half = lax.dynamic_slice_in_dim(r3, 2 * lax.axis_index("c"), 2, 0)
    h_own = lax.ppermute(half, ("z", "c"), ring)
    g3 = lax.ppermute(r3, "c", SWAP)
    step = prev.two()
    h_own = after(h_own, g3, step)
    h_other = lax.ppermute(h_own, "c", SWAP)
    mine, dt_raw = call(
        k_project_late, (wide, sds((T, 128), F32)), "project_late", 0, (hidden, early, r3, g3, h_own, h_other), us=2, limit=20
    )

    pair = lax.ppermute(mine, "y", [(i, i ^ 1) for i in range(4)])
    step = prev.four()
    pair = after(pair, step)
    args = (seg_next, dt_raw, decay_row, bias_row, mine, pair, values)
    local = call(k_local_next, LOCAL_OUTS + (wide, wide), "local_next", 1, args, [pltpu.VMEM((2, 528, 128), F32)], us=3)
    nxt = Scan(False, "_next", local[0], local[1])
    parts_next, bc_next = local[2:6], (local[6], local[7])
    nxt.core()
    base_next = inside(False, "_next", seg_next, skip, parts_next, values, bc_next)
    nxt.send_q = after(nxt.send_q, step)
    nxt.chip()
    step = prev.slab()
    nxt.plane = after(nxt.plane, base_next)
    nxt.two()
    base_prev = inside(True, "_prev", seg_prev, skip, parts_prev, grads, (bc_prev,))
    state_prev = prev.state()
    nxt.pair_send = after(nxt.pair_send, step, base_prev)
    nxt.four()
    nxt.out_q = after(nxt.out_q, state_prev[1])
    grad_values = final(True, "_prev", base_prev, parts_prev[3], state_prev, (bc_prev,))
    nxt.slab()
    nxt.out_h = after(nxt.out_h, grad_values)
    out_next = final(False, "_next", base_next, parts_next[3], nxt.state(), bc_next)
    return out_next, grad_values


def solution(mesh):
    split = Mesh(mesh.devices.reshape(8, 2, 2, 2, 4), ("z", "xl", "c", "xh", "y"))
    all_axes = SEQ + FSDP
    in_specs = (
        P(SEQ, None),
        P(SEQ, FSDP),
        P(),
        P(all_axes, None),
        P(all_axes, None),
        P(),
        P(),
        P(),
        P(SEQ, None),
        P(SEQ, FSDP),
        P(),
        P(SEQ, FSDP),
    )
    out_specs = (P(SEQ, FSDP), P(SEQ, FSDP))
    return jax.shard_map(body, mesh=split, in_specs=in_specs, out_specs=out_specs, check_vma=False)
```

time: 153 us -> 114 us (0.75)
  Pallas kernels: 47.7 us -> 15 us
  waiting for transfers between devices: 13 us -> 29.7 us
  local copies, waits for them, and re-layouts: 20 us -> 10.1 us
  starting transfers between devices: 51.7 us -> 43.4 us
  between operations: 4.66 us -> 0.99 us
    pallas_call x10 -> x0, Pallas kernels: 28 us -> none  [call_scratch(): pl.pallas_call(kernel, out_shape=outs, in_specs=[SM] * n_smem + [VM] * (l...]
    ppermute x25, waiting for transfers between devices: 13 us -> 29.7 us  [the longest x2 7.74 us: four(): older = lax.ppermute(self.pair_send, 'z', along(2, self.reverse))]
    ppermute x25, starting transfers between devices: 51.5 us -> 42.9 us  [the longest x2 7.97 us: two(): self.far = lax.ppermute(self.plane, 'z', along(2, self.reverse))]
    pallas_call x10 -> x21, Pallas kernels: 19.7 us -> 15 us  [call(): pl.pallas_call(kernel, out_shape=outs, in_specs=[SM] * n_smem + [VM] * (l...]
    another operation x6 -> x0, local copies, waits for them, and re-layouts: 4.12 us -> none  [the longest x2 2.68 us: scalars(): return jnp.stack([b0, b1, b2, slab * T, c, x, z, k]).astype(jnp.int32)]
    slice x2 -> x0, local copies, waits for them, and re-layouts: 2.73 us -> none  [scalars(): b2 = b1 + lengths[2]]
    dynamic_slice x3 -> x1, local copies, waits for them, and re-layouts: 1.62 us -> 0.01 us  [body(): half = lax.dynamic_slice_in_dim(r3, 2 * lax.axis_index('c'), 2, 0)]
    unnamed x54 -> x34, local copies, waits for them, and re-layouts: 11.6 us -> 10.1 us
  transfers between devices with their start and end apart: 26 -> 26, of which waited for: 5 -> 14; matrix products, arithmetic and copies ran while one was open for 4% -> 0% of each run, Pallas kernels for 23% -> 9%
where the time goes in v2:
time: 114 us; the launch traced here: 113 us
  starting transfers between devices  43.4 us (38%)
  waiting for transfers between devices  29.7 us (26%)
  Pallas kernels  15 us (13%)
  blocking collectives  14.2 us (12%)
  local copies, waits for them, and re-layouts  10.1 us (9%)
    pallas_call x21, Pallas kernels, call(): pl.pallas_call(kernel, out_shape=outs, in_specs=[SM] * n_smem + [VM] * (l...  15 us
    all_to_all x1, blocking collectives, body(): got = lax.all_to_all(send, FSDP, 0, 0, tiled=False)  14.2 us
    unnamed x34, local copies, waits for them, and re-layouts  10.1 us
    ppermute x2, starting transfers between devices, two(): self.far = lax.ppermute(self.plane, 'z', along(2, self.reverse))  7.97 us
    ppermute x2, waiting for transfers between devices, four(): older = lax.ppermute(self.pair_send, 'z', along(2, self.reverse))  7.74 us
    ppermute x2, starting transfers between devices, four(): older = lax.ppermute(self.pair_send, 'z', along(2, self.reverse))  6.52 us
    ppermute x1, starting transfers between devices, body(): r1 = lax.ppermute(q0, ('z', 'c'), ring)  5.65 us
    ppermute x2, starting transfers between devices, state(): return (self.keep_h, lax.ppermute(self.out_h, 'c', SWAP))  4.67 us
  transfers between devices with their start and end apart: 26, of which 14 were waited for; matrix products, arithmetic and copies ran while one was open for 0% of the time, Pallas kernels for 9%

profile of v2, /device:TPU:1, one launch (start us, length us, event | category | flops | bytes accessed | tf_op | source)
XLA Modules:
  0.0 113.3 jit_solution(6457051909815075502)
XLA Ops:
  2.3 14.2 %all_to_all.5.rec_ref = bf16[8,64,128]{2,1,0:T(8,128)(2,1)S(1)} all-to-all(bf16[8,64,128]{2,1,0:T(8,128)(2,1)S(1)} %columns.1), channel_id=1, replica_groups=mesh['z'=8,'xl'=2,'c'=2,'xh'=2,'y'=4] {'xh','y'}, dimensions={0} | all-to-all | bytes 262144 | tf_op jit(solution)/shard_map/all_to_all | solution.py:442
  16.9 2.9 %collective-permute-done.other_x = bf16[288,128]{1,0:T(8,128)(2,1)S(1)} collective-permute-done((bf16[288,128]{1,0:T(8,128)(2,1)S(1)}, bf16[288,128]{1,0:T(8,128)(2,1)S(1)}, u32[]{:S(2)}, u32[]{:S(2)}) %collective-permute-start) | collective-permute-done | bytes 73760 | tf_op jit(solution)/shard_map/ppermute | solution.py:445
  19.8 3.3 %collective-permute-start.2 = (bf16[288,128]{1,0:T(8,128)(2,1)S(1)}, bf16[288,128]{1,0:T(8,128)(2,1)S(1)}, u32[]{:S(2)}, u32[]{:S(2)}) collective-permute-start(bf16[288,128]{1,0:T(8,128)(2,1)S(1)} %collective-permute-done.other_x), channel_id=1, source_target_pairs={{0,8},{8,0},{1,9},{9,1},{2,10},{10,2},{3,11},{11,3},{4,12},{12,4},... | collective-permute-start | bytes 221192 | tf_op jit(solution)/shard_map/ppermute | solution.py:447
  27.2 2.7 %local_prev.1 = (f32[528,128]{1,0:T(8,128)S(1)}, bf16[528,128]{1,0:T(8,128)(2,1)S(1)}, f32[256,128]{1,0:T(8,128)S(1)}, f32[16,256]{1,0:T(8,128)S(1)}, f32[16,256]{1,0:T(8,128)S(1)}, /*index=5*/f32[256,128]{1,0:T(8,128)S(1)}) custom-call(s32[4]{0:T(128)S(1)} %copy-done.13, f32[16,256]{1,0:T(8,128)S(1)} %bitcast.3, f32[1,128]{1,0:T(1,128)S(1)} %bitcast.4, ...), custom_call_target="tpu_custom_call" | custom-call | flops 30000000 | bytes 300000 | tf_op jit(solution)/shard_map/local_prev/pallas_call | solution.py:23
  29.9 5.7 %collective-permute-start.3 = (bf16[4,288,128]{2,1,0:T(8,128)(2,1)S(1)}, bf16[4,288,128]{2,1,0:T(8,128)(2,1)S(1)}, u32[]{:S(2)}, u32[]{:S(2)}) collective-permute-start(bf16[4,288,128]{2,1,0:T(8,128)(2,1)S(1)} %quad.1.q0), channel_id=1, source_target_pairs={{0,32},{32,64},{64,96},{96,128},{128,160},{160,192},{192,224},{224... | collective-permute-start | bytes 884744 | tf_op jit(solution)/shard_map/ppermute | solution.py:455
  37.0 2.2 %collective-permute-done.3.r1 = bf16[4,288,128]{2,1,0:T(8,128)(2,1)S(1)} collective-permute-done((bf16[4,288,128]{2,1,0:T(8,128)(2,1)S(1)}, bf16[4,288,128]{2,1,0:T(8,128)(2,1)S(1)}, u32[]{:S(2)}, u32[]{:S(2)}) %collective-permute-start.3) | collective-permute-done | bytes 294944 | tf_op jit(solution)/shard_map/ppermute | solution.py:455
  39.2 1.8 %collective-permute-start.5 = (bf16[4,288,128]{2,1,0:T(8,128)(2,1)S(1)}, bf16[4,288,128]{2,1,0:T(8,128)(2,1)S(1)}, u32[]{:S(2)}, u32[]{:S(2)}) collective-permute-start(bf16[4,288,128]{2,1,0:T(8,128)(2,1)S(1)} %collective-permute-done.3.r1), channel_id=1, source_target_pairs={{0,8},{8,0},{1,9},{9,1},{2,10},{10,2},{3,11},{11,3},{4,12},{12,4},... | collective-permute-start | bytes 884744 | tf_op jit(solution)/shard_map/ppermute | solution.py:459
  41.0 1.7 %collective-permute-start.6 = (bf16[4,288,128]{2,1,0:T(8,128)(2,1)S(1)}, bf16[4,288,128]{2,1,0:T(8,128)(2,1)S(1)}, u32[]{:S(2)}, u32[]{:S(2)}) collective-permute-start(bf16[4,288,128]{2,1,0:T(8,128)(2,1)S(1)} %collective-permute-done.3.r1), channel_id=1, source_target_pairs={{0,32},{32,64},{64,96},{96,128},{128,160},{160,192},{192,224},{224... | collective-permute-start | bytes 884744 | tf_op jit(solution)/shard_map/ppermute | solution.py:458
  43.1 3.1 %collective-permute-done.7.got = bf16[272,128]{1,0:T(8,128)(2,1)S(1)} collective-permute-done((bf16[272,128]{1,0:T(8,128)(2,1)S(1)}, bf16[272,128]{1,0:T(8,128)(2,1)S(1)}, u32[]{:S(2)}, u32[]{:S(2)}) %collective-permute-start.7) | collective-permute-done | bytes 69664 | tf_op jit(solution)/shard_map/ppermute | solution.py:398
  46.9 2.1 %collective-permute-start.8 = (bf16[4,288,128]{2,1,0:T(8,128)(2,1)S(1)}, bf16[4,288,128]{2,1,0:T(8,128)(2,1)S(1)}, u32[]{:S(2)}, u32[]{:S(2)}) collective-permute-start(bf16[4,288,128]{2,1,0:T(8,128)(2,1)S(1)} %collective-permute-done.6.r2), channel_id=1, source_target_pairs={{0,8},{8,0},{1,9},{9,1},{2,10},{10,2},{3,11},{11,3},{4,12},{12,4},... | collective-permute-start | bytes 884744 | tf_op jit(solution)/shard_map/ppermute | solution.py:463
  50.2 2.2 %copy-done = bf16[256,8192]{1,0:T(8,128)(2,1)S(1)} copy-done((bf16[256,8192]{1,0:T(8,128)(2,1)S(1)}, bf16[256,8192]{1,0:T(8,128)(2,1)}, u32[]{:S(2)}) %copy-start) | copy-done | bytes 4194328
  54.9 2.1 %collective-permute-start.10 = (bf16[4,288,128]{2,1,0:T(8,128)(2,1)S(1)}, bf16[4,288,128]{2,1,0:T(8,128)(2,1)S(1)}, u32[]{:S(2)}, u32[]{:S(2)}) collective-permute-start(bf16[4,288,128]{2,1,0:T(8,128)(2,1)S(1)} %collective-permute-done.9.r3), channel_id=1, source_target_pairs={{0,8},{8,0},{1,9},{9,1},{2,10},{10,2},{3,11},{11,3},{4,12},{12,4},... | collective-permute-start | bytes 884744 | tf_op jit(solution)/shard_map/ppermute | solution.py:468
  59.6 3.0 %collective-permute-done.12.near = bf16[272,128]{1,0:T(8,128)(2,1)S(1)} collective-permute-done((bf16[272,128]{1,0:T(8,128)(2,1)S(1)}, bf16[272,128]{1,0:T(8,128)(2,1)S(1)}, u32[]{:S(2)}, u32[]{:S(2)}) %collective-permute-start.12) | collective-permute-done | bytes 69664 | tf_op jit(solution)/shard_map/ppermute | solution.py:403
  62.7 3.0 %collective-permute-done.13.far = bf16[272,128]{1,0:T(8,128)(2,1)S(1)} collective-permute-done((bf16[272,128]{1,0:T(8,128)(2,1)S(1)}, bf16[272,128]{1,0:T(8,128)(2,1)S(1)}, u32[]{:S(2)}, u32[]{:S(2)}) %collective-permute-start.13) | collective-permute-done | bytes 69664 | tf_op jit(solution)/shard_map/ppermute | solution.py:404
  67.2 2.2 %copy-done.1 = bf16[256,8192]{1,0:T(8,128)(2,1)S(1)} copy-done((bf16[256,8192]{1,0:T(8,128)(2,1)S(1)}, bf16[256,8192]{1,0:T(8,128)(2,1)}, u32[]{:S(2)}) %copy-start.1) | copy-done | bytes 4194328
  70.7 6.4 %collective-permute-done.16.older = bf16[256,128]{1,0:T(8,128)(2,1)S(1)} collective-permute-done((bf16[256,128]{1,0:T(8,128)(2,1)S(1)}, bf16[256,128]{1,0:T(8,128)(2,1)S(1)}, u32[]{:S(2)}, u32[]{:S(2)}) %collective-permute-start.16) | collective-permute-done | bytes 65568 | tf_op jit(solution)/shard_map/ppermute | solution.py:409
  77.2 2.7 %local_next.1 = (f32[528,128]{1,0:T(8,128)S(1)}, bf16[528,128]{1,0:T(8,128)(2,1)S(1)}, f32[256,128]{1,0:T(8,128)S(1)}, f32[16,256]{1,0:T(8,128)S(1)}, f32[16,256...) custom-call(s32[4]{0:T(128)S(1)} %copy-done.12, ...), custom_call_target="tpu_custom_call" | custom-call | flops 30000000 | bytes 300000 | tf_op jit(solution)/shard_map/local_next/pallas_call | solution.py:23
  83.2 2.1 %inside_next.1.base_ref = f32[256,1024]{1,0:T(8,128)S(1)} custom-call(s32[4]{0:T(128)S(1)} %copy-done.12, f32[128]{0:T(128)S(1)} %copy-done.15, f32[256,128]{1,0:T(8,128)S(1)} %get-tuple-element.62.cum_ref, f32[16,256]{1,0:T(8,128)S(1)} %get-tuple-element.63.cumt_ref, f32[16,256]{1,0:T(8,128)S(1)} %get-tuple-element.64.dtt_ref, ...), custom_call_target="tpu_custom_call" | custom-call | flops 30000000 | bytes 300000 | tf_op jit(solution)/shard_map/inside_next/pallas_call | solution.py:23
  85.4 1.9 %collective-permute-start.19 = (bf16[272,128]{1,0:T(8,128)(2,1)S(1)}, bf16[272,128]{1,0:T(8,128)(2,1)S(1)}, u32[]{:S(2)}, u32[]{:S(2)}) collective-permute-start(bf16[272,128]{1,0:T(8,128)(2,1)S(1)} %chip_next.1), channel_id=1, source_target_pairs={{0,32},{32,64},{64,96},{96,128},{128,160},{160,192},{192,224},{1,3... | collective-permute-start | bytes 208904 | tf_op jit(solution)/shard_map/ppermute | solution.py:403
  87.2 6.7 %collective-permute-start.20 = (bf16[272,128]{1,0:T(8,128)(2,1)S(1)}, bf16[272,128]{1,0:T(8,128)(2,1)S(1)}, u32[]{:S(2)}, u32[]{:S(2)}) collective-permute-start(bf16[272,128]{1,0:T(8,128)(2,1)S(1)} %chip_next.1), channel_id=1, source_target_pairs={{0,64},{32,96},{64,128},{96,160},{128,192},{160,224},{1,65},{33,97... | collective-permute-start | bytes 208904 | tf_op jit(solution)/shard_map/ppermute | solution.py:404
  94.1 2.4 %collective-permute-start.23 = (bf16[512,128]{1,0:T(8,128)(2,1)S(1)}, bf16[512,128]{1,0:T(8,128)(2,1)S(1)}, u32[]{:S(2)}, u32[]{:S(2)}) collective-permute-start(bf16[512,128]{1,0:T(8,128)(2,1)S(1)} %get-tuple-element.77), channel_id=1, source_target_pairs={{0,8},{8,0},{1,9},{9,1},{2,10},{10,2},{3,11},{11,3},{4,12},{12,4},... | collective-permute-start | bytes 393224 | tf_op jit(solution)/shard_map/ppermute | solution.py:421
  96.5 2.1 %inside_prev.1.base_ref = f32[256,1024]{1,0:T(8,128)S(1)} custom-call(s32[4]{0:T(128)S(1)} %copy-done.14, f32[128]{0:T(128)S(1)} %copy-done.15, f32[256,128]{1,0:T(8,128)S(1)} %get-tuple-element.78.cum_ref, f32[16,256]{1,0:T(8,128)S(1)} %get-tuple-element.79.cumt_ref, f32[16,256]{1,0:T(8,128)S(1)} %get-tuple-element.80.dtt_ref, ...), custom_call_target="tpu_custom_call" | custom-call | flops 30000000 | bytes 300000 | tf_op jit(solution)/shard_map/inside_prev/pallas_call | solution.py:23
  98.6 5.2 %collective-permute-start.22 = (bf16[256,128]{1,0:T(8,128)(2,1)S(1)}, bf16[256,128]{1,0:T(8,128)(2,1)S(1)}, u32[]{:S(2)}, u32[]{:S(2)}) collective-permute-start(bf16[256,128]{1,0:T(8,128)(2,1)S(1)} %get-tuple-element.81), channel_id=1, source_target_pairs={{0,64},{32,96},{64,128},{96,160},{128,192},{160,224},{1,65},{33,97... | collective-permute-start | bytes 196616 | tf_op jit(solution)/shard_map/ppermute | solution.py:409
  108.6 2.3 %collective-permute-start.25 = (bf16[512,128]{1,0:T(8,128)(2,1)S(1)}, bf16[512,128]{1,0:T(8,128)(2,1)S(1)}, u32[]{:S(2)}, u32[]{:S(2)}) collective-permute-start(bf16[512,128]{1,0:T(8,128)(2,1)S(1)} %get-tuple-element.89), channel_id=1, source_target_pairs={{0,8},{8,0},{1,9},{9,1},{2,10},{10,2},{3,11},{11,3},{4,12},{12,4},... | collective-permute-start | bytes 393224 | tf_op jit(solution)/shard_map/ppermute | solution.py:421
  (85 shorter events, 28.6 us)
Async XLA Ops:
  16.5 3.3 %collective-permute-start = (bf16[288,128]{1,0:T(8,128)(2,1)S(1)}, bf16[288,128]{1,0:T(8,128)(2,1)S(1)}, u32[]{:S(2)}, u32[]{:S(2)}) collective-permute-start(bf16[288,128]{1,0:T(8,128)(2,1)S(1)} %rows.1.own), channel_id=1, source_target_pairs={{0,16},{16,0},{1,17},{17,1},{2,18},{18,2},{3,19},{19,3},{4,20},{20... | collective-permute-start | bytes 221192 | tf_op jit(solution)/shard_map/ppermute | solution.py:445
  19.8 10.1 %collective-permute-start.2 = (bf16[288,128]{1,0:T(8,128)(2,1)S(1)}, bf16[288,128]{1,0:T(8,128)(2,1)S(1)}, u32[]{:S(2)}, u32[]{:S(2)}) collective-permute-start(bf16[288,128]{1,0:T(8,128)(2,1)S(1)} %collective-permute-done.other_x), channel_id=1, source_target_pairs={{0,8},{8,0},{1,9},{9,1},{2,10},{10,2},{3,11},{11,3},{4,12},{12,4},... | collective-permute-start | bytes 221192 | tf_op jit(solution)/shard_map/ppermute | solution.py:447
  23.0 6.8 %collective-permute-start.1 = (bf16[288,128]{1,0:T(8,128)(2,1)S(1)}, bf16[288,128]{1,0:T(8,128)(2,1)S(1)}, u32[]{:S(2)}, u32[]{:S(2)}) collective-permute-start(bf16[288,128]{1,0:T(8,128)(2,1)S(1)} %rows.1.own), channel_id=1, source_target_pairs={{0,8},{8,0},{1,9},{9,1},{2,10},{10,2},{3,11},{11,3},{4,12},{12,4},... | collective-permute-start | bytes 221192 | tf_op jit(solution)/shard_map/ppermute | solution.py:446
  29.9 9.3 %collective-permute-start.3 = (bf16[4,288,128]{2,1,0:T(8,128)(2,1)S(1)}, bf16[4,288,128]{2,1,0:T(8,128)(2,1)S(1)}, u32[]{:S(2)}, u32[]{:S(2)}) collective-permute-start(bf16[4,288,128]{2,1,0:T(8,128)(2,1)S(1)} %quad.1.q0), channel_id=1, source_target_pairs={{0,32},{32,64},{64,96},{96,128},{128,160},{160,192},{192,224},{224... | collective-permute-start | bytes 884744 | tf_op jit(solution)/shard_map/ppermute | solution.py:455
  39.2 7.1 %collective-permute-start.5 = (bf16[4,288,128]{2,1,0:T(8,128)(2,1)S(1)}, bf16[4,288,128]{2,1,0:T(8,128)(2,1)S(1)}, u32[]{:S(2)}, u32[]{:S(2)}) collective-permute-start(bf16[4,288,128]{2,1,0:T(8,128)(2,1)S(1)} %collective-permute-done.3.r1), channel_id=1, source_target_pairs={{0,8},{8,0},{1,9},{9,1},{2,10},{10,2},{3,11},{11,3},{4,12},{12,4},... | collective-permute-start | bytes 884744 | tf_op jit(solution)/shard_map/ppermute | solution.py:459
  41.0 5.9 %collective-permute-start.6 = (bf16[4,288,128]{2,1,0:T(8,128)(2,1)S(1)}, bf16[4,288,128]{2,1,0:T(8,128)(2,1)S(1)}, u32[]{:S(2)}, u32[]{:S(2)}) collective-permute-start(bf16[4,288,128]{2,1,0:T(8,128)(2,1)S(1)} %collective-permute-done.3.r1), channel_id=1, source_target_pairs={{0,32},{32,64},{64,96},{96,128},{128,160},{160,192},{192,224},{224... | collective-permute-start | bytes 884744 | tf_op jit(solution)/shard_map/ppermute | solution.py:458
  42.8 3.5 %collective-permute-start.7 = (bf16[272,128]{1,0:T(8,128)(2,1)S(1)}, bf16[272,128]{1,0:T(8,128)(2,1)S(1)}, u32[]{:S(2)}, u32[]{:S(2)}) collective-permute-start(bf16[272,128]{1,0:T(8,128)(2,1)S(1)} %get-tuple-element.50), channel_id=1, source_target_pairs={{0,16},{16,0},{1,17},{17,1},{2,18},{18,2},{3,19},{19,3},{4,20},{20... | collective-permute-start | bytes 208904 | tf_op jit(solution)/shard_map/ppermute | solution.py:398
  46.9 3.3 %collective-permute-start.8 = (bf16[4,288,128]{2,1,0:T(8,128)(2,1)S(1)}, bf16[4,288,128]{2,1,0:T(8,128)(2,1)S(1)}, u32[]{:S(2)}, u32[]{:S(2)}) collective-permute-start(bf16[4,288,128]{2,1,0:T(8,128)(2,1)S(1)} %collective-permute-done.6.r2), channel_id=1, source_target_pairs={{0,8},{8,0},{1,9},{9,1},{2,10},{10,2},{3,11},{11,3},{4,12},{12,4},... | collective-permute-start | bytes 884744 | tf_op jit(solution)/shard_map/ppermute | solution.py:463
  49.0 5.9 %collective-permute-start.9 = (bf16[4,288,128]{2,1,0:T(8,128)(2,1)S(1)}, bf16[4,288,128]{2,1,0:T(8,128)(2,1)S(1)}, u32[]{:S(2)}, u32[]{:S(2)}) collective-permute-start(bf16[4,288,128]{2,1,0:T(8,128)(2,1)S(1)} %collective-permute-done.6.r2), channel_id=1, source_target_pairs={{0,32},{32,64},{64,96},{96,128},{128,160},{160,192},{192,224},{224... | collective-permute-start | bytes 884744 | tf_op jit(solution)/shard_map/ppermute | solution.py:462
  54.9 10.8 %collective-permute-start.10 = (bf16[4,288,128]{2,1,0:T(8,128)(2,1)S(1)}, bf16[4,288,128]{2,1,0:T(8,128)(2,1)S(1)}, u32[]{:S(2)}, u32[]{:S(2)}) collective-permute-start(bf16[4,288,128]{2,1,0:T(8,128)(2,1)S(1)} %collective-permute-done.9.r3), channel_id=1, source_target_pairs={{0,8},{8,0},{1,9},{9,1},{2,10},{10,2},{3,11},{11,3},{4,12},{12,4},... | collective-permute-start | bytes 884744 | tf_op jit(solution)/shard_map/ppermute | solution.py:468
  56.9 8.7 %collective-permute-start.11 = (bf16[2,288,128]{2,1,0:T(8,128)(2,1)S(1)}, bf16[2,288,128]{2,1,0:T(8,128)(2,1)S(1)}, u32[]{:S(2)}, u32[]{:S(2)}) collective-permute-start(bf16[2,288,128]{2,1,0:T(8,128)(2,1)S(1)} %constant_dynamic-slice_fusion), channel_id=1, source_target_pairs={{0,32},{32,64},{64,96},{96,128},{128,160},{160,192},{192,224},{224... | collective-permute-start | bytes 442376 | tf_op jit(solution)/shard_map/ppermute | solution.py:467
  57.0 5.6 %collective-permute-start.12 = (bf16[272,128]{1,0:T(8,128)(2,1)S(1)}, bf16[272,128]{1,0:T(8,128)(2,1)S(1)}, u32[]{:S(2)}, u32[]{:S(2)}) collective-permute-start(bf16[272,128]{1,0:T(8,128)(2,1)S(1)} %chip_prev.1), channel_id=1, source_target_pairs={{32,0},{64,32},{96,64},{128,96},{160,128},{192,160},{224,192},{33,... | collective-permute-start | bytes 208904 | tf_op jit(solution)/shard_map/ppermute | solution.py:403
  58.3 7.3 %collective-permute-start.13 = (bf16[272,128]{1,0:T(8,128)(2,1)S(1)}, bf16[272,128]{1,0:T(8,128)(2,1)S(1)}, u32[]{:S(2)}, u32[]{:S(2)}) collective-permute-start(bf16[272,128]{1,0:T(8,128)(2,1)S(1)} %chip_prev.1), channel_id=1, source_target_pairs={{64,0},{96,32},{128,64},{160,96},{192,128},{224,160},{65,1},{97,33... | collective-permute-start | bytes 208904 | tf_op jit(solution)/shard_map/ppermute | solution.py:404
  65.9 11.2 %collective-permute-start.16 = (bf16[256,128]{1,0:T(8,128)(2,1)S(1)}, bf16[256,128]{1,0:T(8,128)(2,1)S(1)}, u32[]{:S(2)}, u32[]{:S(2)}) collective-permute-start(bf16[256,128]{1,0:T(8,128)(2,1)S(1)} %get-tuple-element.55), channel_id=1, source_target_pairs={{64,0},{96,32},{128,64},{160,96},{192,128},{224,160},{65,1},{97,33... | collective-permute-start | bytes 196616 | tf_op jit(solution)/shard_map/ppermute | solution.py:409
  70.2 7.0 %collective-permute-start.15 = (bf16[256,128]{1,0:T(8,128)(2,1)S(1)}, bf16[256,128]{1,0:T(8,128)(2,1)S(1)}, u32[]{:S(2)}, u32[]{:S(2)}) collective-permute-start(bf16[256,128]{1,0:T(8,128)(2,1)S(1)} %get-tuple-element.58.mine_ref), channel_id=1, source_target_pairs={{0,1},{1,0},{2,3},{3,2},{4,5},{5,4},{6,7},{7,6},{8,9},{9,8},{10,11... | collective-permute-start | bytes 196616 | tf_op jit(solution)/shard_map/ppermute | solution.py:476
  79.9 1.7 %collective-permute-start.17 = (bf16[528,128]{1,0:T(8,128)(2,1)S(1)}, bf16[528,128]{1,0:T(8,128)(2,1)S(1)}, u32[]{:S(2)}, u32[]{:S(2)}) collective-permute-start(bf16[528,128]{1,0:T(8,128)(2,1)S(1)} %get-tuple-element.69), channel_id=1, source_target_pairs={{0,8},{8,0},{1,9},{9,1},{2,10},{10,2},{3,11},{11,3},{4,12},{12,4},... | collective-permute-start | bytes 405512 | tf_op jit(solution)/shard_map/ppermute | solution.py:393
  81.7 3.6 %collective-permute-start.18 = (bf16[272,128]{1,0:T(8,128)(2,1)S(1)}, bf16[272,128]{1,0:T(8,128)(2,1)S(1)}, u32[]{:S(2)}, u32[]{:S(2)}) collective-permute-start(bf16[272,128]{1,0:T(8,128)(2,1)S(1)} %get-tuple-element.72), channel_id=1, source_target_pairs={{0,16},{16,0},{1,17},{17,1},{2,18},{18,2},{3,19},{19,3},{4,20},{20... | collective-permute-start | bytes 208904 | tf_op jit(solution)/shard_map/ppermute | solution.py:398
  82.1 11.8 %collective-permute-start.21 = (bf16[256,128]{1,0:T(8,128)(2,1)S(1)}, bf16[256,128]{1,0:T(8,128)(2,1)S(1)}, u32[]{:S(2)}, u32[]{:S(2)}) collective-permute-start(bf16[256,128]{1,0:T(8,128)(2,1)S(1)} %get-tuple-element.60), channel_id=1, source_target_pairs={{0,16},{16,0},{1,17},{17,1},{2,18},{18,2},{3,19},{19,3},{4,20},{20... | collective-permute-start | bytes 196616 | tf_op jit(solution)/shard_map/ppermute | solution.py:415
  85.4 13.2 %collective-permute-start.19 = (bf16[272,128]{1,0:T(8,128)(2,1)S(1)}, bf16[272,128]{1,0:T(8,128)(2,1)S(1)}, u32[]{:S(2)}, u32[]{:S(2)}) collective-permute-start(bf16[272,128]{1,0:T(8,128)(2,1)S(1)} %chip_next.1), channel_id=1, source_target_pairs={{0,32},{32,64},{64,96},{96,128},{128,160},{160,192},{192,224},{1,3... | collective-permute-start | bytes 208904 | tf_op jit(solution)/shard_map/ppermute | solution.py:403
  87.2 11.4 %collective-permute-start.20 = (bf16[272,128]{1,0:T(8,128)(2,1)S(1)}, bf16[272,128]{1,0:T(8,128)(2,1)S(1)}, u32[]{:S(2)}, u32[]{:S(2)}) collective-permute-start(bf16[272,128]{1,0:T(8,128)(2,1)S(1)} %chip_next.1), channel_id=1, source_target_pairs={{0,64},{32,96},{64,128},{96,160},{128,192},{160,224},{1,65},{33,97... | collective-permute-start | bytes 208904 | tf_op jit(solution)/shard_map/ppermute | solution.py:404
  94.1 11.2 %collective-permute-start.23 = (bf16[512,128]{1,0:T(8,128)(2,1)S(1)}, bf16[512,128]{1,0:T(8,128)(2,1)S(1)}, u32[]{:S(2)}, u32[]{:S(2)}) collective-permute-start(bf16[512,128]{1,0:T(8,128)(2,1)S(1)} %get-tuple-element.77), channel_id=1, source_target_pairs={{0,8},{8,0},{1,9},{9,1},{2,10},{10,2},{3,11},{11,3},{4,12},{12,4},... | collective-permute-start | bytes 393224 | tf_op jit(solution)/shard_map/ppermute | solution.py:421
  98.6 6.6 %collective-permute-start.22 = (bf16[256,128]{1,0:T(8,128)(2,1)S(1)}, bf16[256,128]{1,0:T(8,128)(2,1)S(1)}, u32[]{:S(2)}, u32[]{:S(2)}) collective-permute-start(bf16[256,128]{1,0:T(8,128)(2,1)S(1)} %get-tuple-element.81), channel_id=1, source_target_pairs={{0,64},{32,96},{64,128},{96,160},{128,192},{160,224},{1,65},{33,97... | collective-permute-start | bytes 196616 | tf_op jit(solution)/shard_map/ppermute | solution.py:409
  105.2 3.2 %collective-permute-start.24 = (bf16[256,128]{1,0:T(8,128)(2,1)S(1)}, bf16[256,128]{1,0:T(8,128)(2,1)S(1)}, u32[]{:S(2)}, u32[]{:S(2)}) collective-permute-start(bf16[256,128]{1,0:T(8,128)(2,1)S(1)} %get-tuple-element.84), channel_id=1, source_target_pairs={{0,16},{16,0},{1,17},{17,1},{2,18},{18,2},{3,19},{19,3},{4,20},{20... | collective-permute-start | bytes 196616 | tf_op jit(solution)/shard_map/ppermute | solution.py:415
  108.6 3.3 %collective-permute-start.25 = (bf16[512,128]{1,0:T(8,128)(2,1)S(1)}, bf16[512,128]{1,0:T(8,128)(2,1)S(1)}, u32[]{:S(2)}, u32[]{:S(2)}) collective-permute-start(bf16[512,128]{1,0:T(8,128)(2,1)S(1)} %get-tuple-element.89), channel_id=1, source_target_pairs={{0,8},{8,0},{1,9},{9,1},{2,10},{10,2},{3,11},{11,3},{4,12},{12,4},... | collective-permute-start | bytes 393224 | tf_op jit(solution)/shard_map/ppermute | solution.py:421
  (19 other events, 224.4 us)

commit v3 on v2

--- a/solution.py
+++ b/solution.py
@@ -53,34 +53,52 @@
 
 
 def k_columns(bc_ref, dt_ref, out_ref):
-    me = fsdp_place()
-    lane = lanes((32, 128))
-    low = lane < 64
+    low = lanes((32, 128)) < 64
+    parts = []
     for j in range(4):
         b = bc_ref[:, 128 * j : 128 * j + 128].astype(F32)
         c = bc_ref[:, 512 + 128 * j : 640 + 128 * j].astype(F32)
-        out_ref[2 * j, 0:32] = jnp.where(low, b, pltpu.roll(c, 64, 1)).astype(BF)
-        out_ref[2 * j + 1, 0:32] = jnp.where(low, pltpu.roll(b, 64, 1), c).astype(BF)
+        parts.append(jnp.where(low, b, pltpu.roll(c, 64, 1)))
+        parts.append(jnp.where(low, pltpu.roll(b, 64, 1), c))
     d = dt_ref[...].astype(F32)
-    mine = lane // 16 == me
+    diagonal = lanes((8, 128)) // 16 == rows((8, 128))
     for k in range(8):
-        out_ref[k, 32:64] = jnp.where(mine, pltpu.roll(d, (16 * (me - k)) & 127, 1), 0.0).astype(BF)
+        packed = []
+        for q in range(4):
+            piece = jnp.concatenate(
+                [pltpu.roll(d[8 * q : 8 * q + 8], (16 * (i - k)) % 128, 1)[i : i + 1] for i in range(8)], axis=0
+            )
+            packed.append(jnp.sum(jnp.where(diagonal, piece, 0.0), axis=0, keepdims=True))
+        whole = jnp.concatenate([parts[k]] + packed + [jnp.zeros((4, 128), F32)], axis=0)[0:36].astype(BF)
+        for x in range(2):
+            out_ref[x, k] = whole
 
 
 def k_rows(rec_ref, out_ref):
-    total = jnp.zeros((32, 128), F32)
-    for k in range(8):
-        out_ref[32 * k : 32 * k + 32] = rec_ref[k, 0:32]
-        total = total + rec_ref[k, 32:64].astype(F32)
-    out_ref[256:288] = total.astype(BF)
-
-
-def k_quad(own, other_x, other_c, other_xc, out_ref):
-    c, x = lax.axis_index("c"), lax.axis_index("xl")
-    out_ref[2 * x + c] = own[...]
-    out_ref[2 * (1 - x) + c] = other_x[...]
-    out_ref[2 * x + 1 - c] = other_c[...]
-    out_ref[2 * (1 - x) + 1 - c] = other_xc[...]
+    group = lanes((8, 128)) // 16
+    sub = rows((8, 128))
+    for x in range(2):
+        for m in range(8):
+            out_ref[x, 32 * m : 32 * m + 32] = rec_ref[8 * x + m, 0:32]
+        tails = [rec_ref[8 * x + m, 32:36].astype(F32) for m in range(8)]
+        done = []
+        for q in range(4):
+            a = jnp.concatenate([t[q : q + 1] for t in tails], axis=0)
+            out = jnp.zeros((8, 128), F32)
+            for d in range(8):
+                moved = pltpu.roll(pltpu.roll(a, (8 - d) % 8, 0), 16 * d, 1)
+                out = jnp.where(group == ((sub + d) & 7), moved, out)
+            done.append(out)
+        out_ref[x, 256:288] = jnp.concatenate(done, axis=0).astype(BF)
+
+
+def k_pack(a, b, out_ref):
+    out_ref[0:2] = a[...]
+    out_ref[2:4] = b[...]
+
+
+def k_load(hid_ref, out_ref):
+    pltpu.sync_copy(hid_ref, out_ref)
 
 
 def weight_block(part):
@@ -90,29 +108,33 @@
     return jnp.concatenate([part[0:256], jnp.where(spread, tall, jnp.zeros_like(tall))], axis=1)
 
 
-def times(hid, off, parts):
-    left = hid[:, pl.ds(pl.multiple_of(off, 256), 256 * len(parts))]
-    right = jnp.concatenate([weight_block(p) for p in parts], axis=0)
-    return jnp.dot(left, right, preferred_element_type=F32)
-
-
-def k_project_early(hid, q0, r1, g1, r2, g2, acc_ref):
-    z, sign = lax.axis_index("z"), 1 - 2 * lax.axis_index("c")
-    acc = times(hid, 1024 * z, [q0[b] for b in range(4)])
-    for r, (up, down) in enumerate(((r1, g1), (r2, g2)), 1):
-        acc = acc + times(hid, 1024 * ((z - sign * r) & 7), [up[b] for b in range(4)])
-        acc = acc + times(hid, 1024 * ((z + sign * r) & 7), [down[b] for b in range(4)])
-    acc_ref[...] = acc
-
-
-def k_project_late(hid, early, r3, g3, h_own, h_other, y_ref, dt_ref):
-    c, z = lax.axis_index("c"), lax.axis_index("z")
-    sign = 1 - 2 * c
-    acc = early[...] + times(hid, 1024 * ((z - sign * 3) & 7), [r3[b] for b in range(4)])
-    acc = acc + times(hid, 1024 * ((z + sign * 3) & 7), [g3[b] for b in range(4)])
-    far = 1024 * ((z + 4) & 7)
-    acc = acc + times(hid, far + 512 * c, [h_own[b] for b in range(2)])
-    acc = acc + times(hid, far + 512 * (1 - c), [h_other[b] for b in range(2)])
+def side_of_pair():
+    return 1 - 2 * ((lax.axis_index("z") + lax.axis_index("c")) & 1)
+
+
+def times(hid, parts, planes, core):
+    left = [
+        hid[:, pl.ds(pl.multiple_of(1024 * (p & 7) + 512 * x + 256 * core, 256), 256)] for p in planes for x in range(2)
+    ]
+    right = jnp.concatenate([weight_block(parts[b]) for b in range(4)], axis=0)
+    return jnp.dot(jnp.concatenate(left, axis=1), right, preferred_element_type=F32)
+
+
+def k_project(step, last, *refs):
+    hid, refs = refs[0], refs[1:]
+    z, c, s = lax.axis_index("z"), lax.axis_index("c"), side_of_pair()
+    acc = None if step[0] == 0 else refs[0][...]
+    if step[0] > 0:
+        refs = refs[1:]
+    for n, at in enumerate(step):
+        first, second = ((0, 1), (-1, -2), (2, 3), (-3, -4))[at]
+        mine = times(hid, refs[2 * n], (z + s * first, z + s * second), c)
+        acc = mine if acc is None else acc + mine
+        acc = acc + times(hid, refs[2 * n + 1], (z - s * first, z - s * second), 1 - c)
+    if not last:
+        refs[-1][...] = acc
+        return
+    y_ref, dt_ref = refs[-2:]
     y_ref[...] = acc[:, 0:128].astype(BF)
     d = acc[:, 128:256]
     for shift in (16, 32, 64):
@@ -272,9 +294,9 @@
 
 def k_final(reverse, base_ref, late_ref, keep_ref, got_ref, *refs):
     out_ref, scratch = refs[-2:]
-    core = lax.axis_index("c")
-    scratch[core] = keep_ref[...].astype(BF)
-    scratch[1 - core] = got_ref[...]
+    core, r = lax.axis_index("c"), int(reverse)
+    scratch[core] = keep_ref[r]
+    scratch[1 - core] = got_ref[r]
     low = lanes((T, 128)) < 64
     late = late_ref[...]
     b, c = sides(reverse, refs)
@@ -324,101 +346,113 @@
     send_ref[...] = scratch[1 - x].astype(BF)
 
 
-def k_chip(reverse, own, got, out_ref):
+def chip_sum(reverse, own, got):
     x = lax.axis_index("xl")
     mine_first = first_of(reverse, x)
     so, sg = own[0:256], got[0:256].astype(F32)
     ao, ag = decays_of(own[256:272]), decays_of(got[256:272])
     first, second = jnp.where(mine_first, so, sg), jnp.where(mine_first, sg, so)
     a_second = jnp.where(mine_first, ag, ao)
-    out_ref[0:256] = (second + quarter_rows(a_second, x) * first).astype(BF)
-    out_ref[256:272] = tail_of(ao * ag).astype(BF)
-
-
-def k_two(near, far, keep_ref, send_ref):
+    return second + quarter_rows(a_second, x) * first, tail_of(ao * ag)
+
+
+def k_chip_prev(own, got, out_ref):
+    out_ref[0:256], out_ref[256:272] = chip_sum(True, own, got)
+
+
+def k_chip_next(own, got, prev, out_ref, msg_ref):
+    state, tail = chip_sum(False, own, got)
+    out_ref[0:256], out_ref[256:272] = state, tail
+    msg_ref[0, 0:256], msg_ref[0, 256:272] = state.astype(BF), tail.astype(BF)
+    msg_ref[1] = prev[...].astype(BF)
+
+
+def pair_place():
+    z, c = lax.axis_index("z"), lax.axis_index("c")
+    q = z + c
+    alone = (c == 1) & ((z == 0) | (z == 7))
+    return q // 2, (q & 1) == 1, jnp.logical_not(alone), 3 + c
+
+
+def k_pairs(next_ref, prev_ref, got, out_ref):
     x = lax.axis_index("xl")
-    a = decays_of(near[256:272])
-    two = near[0:256].astype(F32) + quarter_rows(a, x) * far[0:256].astype(F32)
-    keep_ref[...] = two
-    send_ref[...] = two.astype(BF)
-
-
-def k_four(reverse, near, far, pair, older, own, got, keep_ref, send_ref):
+    _, upper, partner, _ = pair_place()
+    sums = []
+    for r, own in enumerate((next_ref, prev_ref)):
+        mine_first = jnp.logical_not(upper) if r == 0 else upper
+        so, ao = own[0:256], decays_of(own[256:272])
+        sg, ag = got[r, 0:256].astype(F32), decays_of(got[r, 256:272])
+        first, second = jnp.where(mine_first, so, sg), jnp.where(mine_first, sg, so)
+        total = second + quarter_rows(jnp.where(mine_first, ag, ao), x) * first
+        sums.append((jnp.where(partner, total, so), tail_of(jnp.where(partner, ao * ag, ao))))
+    out_ref[0:256] = jnp.where(upper, sums[0][0], sums[1][0]).astype(BF)
+    out_ref[256:272] = jnp.where(upper, sums[0][1], sums[1][1]).astype(BF)
+
+
+def k_planes(got, m2, m3, m4, m5, own_n, got_n, own_p, got_p, keep_ref, send_ref):
     x = lax.axis_index("xl")
-    a = decays_of(near[256:272]) * decays_of(far[256:272])
-    before = pair[...] + quarter_rows(a, x) * older[...].astype(F32)
-    mine_first = first_of(reverse, x)
-    first = jnp.where(mine_first, own[0:256], got[0:256].astype(F32))
-    a_first = jnp.where(mine_first, decays_of(own[256:272]), decays_of(got[256:272]))
-    after = first + quarter_rows(a_first, x) * before
-    keep_ref[...] = jnp.where(mine_first, before, after)
-    send_ref[...] = jnp.where(mine_first, after, before).astype(BF)
-
-
-def k_slab(reverse, mine, other, own, got, keep_ref, send_ref, scratch):
+    m, upper, partner, top = pair_place()
+    for r, (own, other) in enumerate(((own_n, got_n), (own_p, got_p))):
+        straight = upper if r == 1 else jnp.logical_not(upper)
+        near_there = (m + 1 <= top) if r == 1 else (m >= 1)
+        far_there = (m + 2 <= top) if r == 1 else (m >= 2)
+        near = jnp.where(straight, m2[...].astype(F32), m3[...].astype(F32))
+        far = jnp.where(straight, m4[0:256].astype(F32), m5[0:256].astype(F32))
+        far = jnp.where(far_there, far, 0.0)
+        total = near[0:256] + quarter_rows(near[256:264] + near[264:272], x) * far
+        total = jnp.where(near_there, total, 0.0)
+        beyond = got[r, 0:256].astype(F32) + quarter_rows(decays_of(got[r, 256:272]), x) * total
+        before = jnp.where(jnp.logical_or(straight, jnp.logical_not(partner)), total, beyond)
+        mine_first = first_of(r == 1, x)
+        first = jnp.where(mine_first, own[0:256], other[0:256].astype(F32))
+        a_first = jnp.where(mine_first, decays_of(own[256:272]), decays_of(other[256:272]))
+        after_x = first + quarter_rows(a_first, x) * before
+        keep_ref[r] = jnp.where(mine_first, before, after_x)
+        send_ref[r] = jnp.where(mine_first, after_x, before).astype(BF)
+
+
+def k_slab(mine, other, own_n, got_n, own_p, got_p, keep_ref, send_ref, scratch):
     core, x = lax.axis_index("c"), lax.axis_index("xl")
-    scratch[x] = mine[...]
-    scratch[1 - x] = other[...].astype(F32)
-    before = jnp.concatenate([scratch[0], scratch[1]], axis=0)
-    mine_first = first_of(reverse, core)
-    first = jnp.where(mine_first, own[0:512], got[0:512].astype(F32))
-    a_first = jnp.where(mine_first, decays_of(own[512:528]), decays_of(got[512:528]))
-    after = first + per_row(a_first, 8) * before
-    keep_ref[...] = jnp.where(mine_first, before, after)
-    send_ref[...] = jnp.where(mine_first, after, before).astype(BF)
-
-
-def along(distance, reverse):
-    if reverse:
-        return [(i, i - distance) for i in range(distance, 8)]
-    return [(i, i + distance) for i in range(8 - distance)]
+    for r, (own, got) in enumerate(((own_n, got_n), (own_p, got_p))):
+        scratch[x] = mine[r]
+        scratch[1 - x] = other[r].astype(F32)
+        before = jnp.concatenate([scratch[0], scratch[1]], axis=0)
+        mine_first = first_of(r == 1, core)
+        first = jnp.where(mine_first, own[0:512], got[0:512].astype(F32))
+        a_first = jnp.where(mine_first, decays_of(own[512:528]), decays_of(got[512:528]))
+        after_c = first + per_row(a_first, 8) * before
+        keep_ref[r] = jnp.where(mine_first, before, after_c).astype(BF)
+        send_ref[r] = jnp.where(mine_first, after_c, before).astype(BF)
 
 
 SWAP = [(0, 1), (1, 0)]
 HALF, QUARTER, TAILED = (512, 128), (256, 128), (272, 128)
 
 
-def both(shape):
-    return sds(shape, F32), sds(shape, BF)
-
-
-class Scan:
-    def __init__(self, reverse, tag, keep, send):
-        self.reverse, self.tag, self.keep, self.send = reverse, tag, keep, send
-
-    def run(self, kernel, outs, name, args, scratch=()):
-        return call(functools.partial(kernel, self.reverse), outs, name + self.tag, 0, args, scratch)
-
-    def core(self):
-        self.got = lax.ppermute(self.send, "c", SWAP)
-        self.own_q, self.send_q = self.run(k_core, both(TAILED), "core", (self.keep, self.got), [pltpu.VMEM((2,) + TAILED, F32)])
-        return self.send_q
-
-    def chip(self):
-        self.got_q = lax.ppermute(self.send_q, "xl", SWAP)
-        self.plane = self.run(k_chip, sds(TAILED, BF), "chip", (self.own_q, self.got_q))
-        return self.plane
-
-    def two(self):
-        self.near = lax.ppermute(self.plane, "z", along(1, self.reverse))
-        self.far = lax.ppermute(self.plane, "z", along(2, self.reverse))
-        self.pair, self.pair_send = call(k_two, both(QUARTER), "two" + self.tag, 0, (self.near, self.far))
-        return self.pair_send
-
-    def four(self):
-        older = lax.ppermute(self.pair_send, "z", along(2, self.reverse))
-        args = (self.near, self.far, self.pair, older, self.own_q, self.got_q)
-        self.keep_q, self.out_q = self.run(k_four, both(QUARTER), "four", args)
-        return self.out_q
-
-    def slab(self):
-        back = lax.ppermute(self.out_q, "xl", SWAP)
-        args = (self.keep_q, back, self.keep, self.got)
-        self.keep_h, self.out_h = self.run(k_slab, both(HALF), "slab", args, [pltpu.VMEM((2,) + QUARTER, F32)])
-        return self.out_h
-
-    def state(self):
-        return self.keep_h, lax.ppermute(self.out_h, "c", SWAP)
+def neighbour(z, x, odd, wrap):
+    if not odd:
+        return z ^ 1, x
+    other = z + 1 if z & 1 else z - 1
+    if wrap:
+        return other % 8, x
+    return (other, x) if 0 <= other < 8 else (z, 1 - x)
+
+
+def along_z(array, step, wrap=False):
+    pairs = []
+    for z in range(8):
+        for x in range(2):
+            for c in range(2):
+                z2, x2 = neighbour(z, x, (step + c) % 2, wrap)
+                pairs.append((4 * z + 2 * x + c, 4 * z2 + 2 * x2 + c))
+    return lax.ppermute(array, SEQ, pairs)
+
+
+def core_sum(reverse, tag, keep, send):
+    got = lax.ppermute(send, "c", SWAP)
+    outs = (sds(TAILED, F32), sds(TAILED, BF))
+    own_q, send_q = call(functools.partial(k_core, reverse), outs, "core" + tag, 0, (keep, got), [pltpu.VMEM((2,) + TAILED, F32)])
+    return got, own_q, send_q
 
 
 def inside(reverse, tag, lengths, skip, parts, values, bc):
@@ -434,68 +468,73 @@
     return call(kernel, sds((T, 1024), BF), "final" + tag, 0, args, [pltpu.VMEM((2, 512, 128), BF)], us=2)
 
 
+def project(name, step, last, args):
+    outs = (sds((T, 128), BF), sds((T, 128), F32)) if last else sds((T, 256), F32)
+    return call(functools.partial(k_project, step, last), outs, name, 0, args, limit=16)
+
+
 def body(hidden, values, seg_next, proj_bc, proj_dt, dt_bias, decay, skip, bc_prev, dt_prev, seg_prev, grads):
     decay_row, bias_row = decay[None, :], dt_bias[None, :]
     wide = sds((T, 128), BF)
 
-    send = call(k_columns, sds((8, 64, 128), BF), "columns", 0, (proj_bc, proj_dt))
-    got = lax.all_to_all(send, FSDP, 0, 0, tiled=False)
-    own = call(k_rows, sds((288, 128), BF), "rows", 0, (got,))
-
-    other_x = lax.ppermute(own, "xl", SWAP)
-    other_c = lax.ppermute(own, "c", SWAP)
-    other_xc = lax.ppermute(other_x, "c", SWAP)
-    args = (after(seg_prev, own), dt_prev.T, decay_row, bc_prev, grads)
+    send = call(k_columns, sds((2, 8, 36, 128), BF), "columns", 0, (proj_bc, proj_dt)).reshape(16, 36, 128)
+    got = lax.all_to_all(send, ("xl",) + FSDP, 0, 0, tiled=False)
+    w0 = call(k_rows, sds((2, 288, 128), BF), "rows", 0, (got,))
+
+    w1 = along_z(w0, 0, True)
+    hid = pl.pallas_call(
+        k_load,
+        out_shape=sds(hidden.shape, BF),
+        in_specs=[pl.BlockSpec(memory_space=pl.ANY)],
+        out_specs=VM,
+        name="load",
+        compiler_params=pltpu.CompilerParams(vmem_limit_bytes=6 << 20),
+        cost_estimate=pl.CostEstimate(flops=30_000_000, bytes_accessed=4_000_000, transcendentals=0),
+    )(after(hidden, w0))
+    args = (after(seg_prev, w0), dt_prev.T, decay_row, bc_prev, grads)
     local = call(k_local_prev, LOCAL_OUTS, "local_prev", 1, args, [pltpu.VMEM((2, 528, 128), F32)], us=3)
-    prev = Scan(True, "_prev", local[0], local[1])
-    parts_prev = local[2:6]
-    q0 = call(k_quad, sds((4, 288, 128), BF), "quad", 0, (own, other_x, other_c, after(other_xc, local[1])))
-
-    ring = [(2 * z, 2 * ((z + 1) % 8)) for z in range(8)] + [(2 * z + 1, 2 * ((z - 1) % 8) + 1) for z in range(8)]
-    r1 = lax.ppermute(q0, ("z", "c"), ring)
-    step = prev.core()
-    r1 = after(r1, step)
-    r2 = lax.ppermute(r1, ("z", "c"), ring)
-    g1 = lax.ppermute(r1, "c", SWAP)
-    step = prev.chip()
-    r2 = after(r2, step, g1)
-    r3 = lax.ppermute(r2, ("z", "c"), ring)
-    g2 = lax.ppermute(r2, "c", SWAP)
-    early = call(k_project_early, sds((T, 256), F32), "project_early", 0, (hidden, q0, r1, g1, r2, g2), us=3, limit=20)
-    r3 = after(r3, early)
-    half = lax.dynamic_slice_in_dim(r3, 2 * lax.axis_index("c"), 2, 0)
-    h_own = lax.ppermute(half, ("z", "c"), ring)
-    g3 = lax.ppermute(r3, "c", SWAP)
-    step = prev.two()
-    h_own = after(h_own, g3, step)
-    h_other = lax.ppermute(h_own, "c", SWAP)
-    mine, dt_raw = call(
-        k_project_late, (wide, sds((T, 128), F32)), "project_late", 0, (hidden, early, r3, g3, h_own, h_other), us=2, limit=20
-    )
+    keep_p, parts_prev = local[0], local[2:6]
+    b0 = call(k_pack, sds((4, 288, 128), BF), "pack", 0, (w0, after(w1, local[1], hid)))
+    b1 = along_z(b0, 1, True)
+    g0 = lax.ppermute(b0, "c", SWAP)
+    got_p, own_qp, send_qp = core_sum(True, "_prev", keep_p, local[1])
+    b1 = after(b1, g0, send_qp)
+    b2 = along_z(b1, 0, True)
+    g1 = lax.ppermute(b1, "c", SWAP)
+    got_qp = lax.ppermute(send_qp, "xl", SWAP)
+    plane_p = call(k_chip_prev, sds(TAILED, F32), "chip_prev", 0, (own_qp, got_qp))
+    acc = project("project0", (0, 1), False, (hid, b0, g0, b1, g1))
+    b2 = after(b2, g1, plane_p, acc)
+    b3 = along_z(b2, 1, True)
+    g2 = lax.ppermute(b2, "c", SWAP)
+    acc = project("project2", (2,), False, (hid, acc, b2, g2))
+    base_prev = inside(True, "_prev", seg_prev, skip, parts_prev, grads, (bc_prev,))
+    b3 = after(b3, acc, base_prev)
+    g3 = lax.ppermute(b3, "c", SWAP)
+    mine, dt_raw = project("project3", (3,), True, (hid, acc, b3, g3))
 
     pair = lax.ppermute(mine, "y", [(i, i ^ 1) for i in range(4)])
-    step = prev.four()
-    pair = after(pair, step)
     args = (seg_next, dt_raw, decay_row, bias_row, mine, pair, values)
     local = call(k_local_next, LOCAL_OUTS + (wide, wide), "local_next", 1, args, [pltpu.VMEM((2, 528, 128), F32)], us=3)
-    nxt = Scan(False, "_next", local[0], local[1])
-    parts_next, bc_next = local[2:6], (local[6], local[7])
-    nxt.core()
+    keep_n, parts_next, bc_next = local[0], local[2:6], (local[6], local[7])
+    got_n, own_qn, send_qn = core_sum(False, "_next", keep_n, local[1])
+    got_qn = lax.ppermute(send_qn, "xl", SWAP)
     base_next = inside(False, "_next", seg_next, skip, parts_next, values, bc_next)
-    nxt.send_q = after(nxt.send_q, step)
-    nxt.chip()
-    step = prev.slab()
-    nxt.plane = after(nxt.plane, base_next)
-    nxt.two()
-    base_prev = inside(True, "_prev", seg_prev, skip, parts_prev, grads, (bc_prev,))
-    state_prev = prev.state()
-    nxt.pair_send = after(nxt.pair_send, step, base_prev)
-    nxt.four()
-    nxt.out_q = after(nxt.out_q, state_prev[1])
-    grad_values = final(True, "_prev", base_prev, parts_prev[3], state_prev, (bc_prev,))
-    nxt.slab()
-    nxt.out_h = after(nxt.out_h, grad_values)
-    out_next = final(False, "_next", base_next, parts_next[3], nxt.state(), bc_next)
+    both = (sds(TAILED, F32), sds((2,) + TAILED, BF))
+    plane_n, msg = call(k_chip_next, both, "chip_next", 0, (own_qn, after(got_qn, base_next), plane_p))
+    m1 = along_z(msg, 0)
+    m = [call(k_pairs, sds(TAILED, BF), "pairs", 0, (plane_n, plane_p, m1))]
+    for step in range(1, 5):
+        m.append(along_z(m[-1], step))
+    both = (sds((2,) + QUARTER, F32), sds((2,) + QUARTER, BF))
+    keep_q, out_q = call(k_planes, both, "planes", 0, (m1, *m[1:], own_qn, got_qn, own_qp, got_qp))
+    back_q = lax.ppermute(out_q, "xl", SWAP)
+    both = (sds((2,) + HALF, BF), sds((2,) + HALF, BF))
+    args = (keep_q, back_q, keep_n, got_n, keep_p, got_p)
+    keep_h, out_h = call(k_slab, both, "slab", 0, args, [pltpu.VMEM((2,) + QUARTER, F32)])
+    state = (keep_h, lax.ppermute(out_h, "c", SWAP))
+    out_next = final(False, "_next", base_next, parts_next[3], state, bc_next)
+    grad_values = final(True, "_prev", base_prev, parts_prev[3], state, (bc_prev,))
     return out_next, grad_values
 
 

time: 114 us -> 101 us (0.89)
  starting transfers between devices: 43.4 us -> 29.2 us
  waiting for transfers between devices: 29.7 us -> 36.2 us
  local copies, waits for them, and re-layouts: 10.1 us -> 4.48 us
    ppermute x25 -> x19, starting transfers between devices: 42.9 us -> 28.7 us  [the longest x9 9.56 us: along_z(): return lax.ppermute(array, SEQ, pairs)]
    unnamed x34 -> x24, local copies, waits for them, and re-layouts: 10.1 us -> 4.48 us
    ppermute x25 -> x19, waiting for transfers between devices: 29.7 us -> 33.3 us  [the longest x9 21.3 us: along_z(): return lax.ppermute(array, SEQ, pairs)]
    ppermute x1, waiting for transfers between devices: 0.01 us -> 2.94 us  [body(): pair = lax.ppermute(mine, 'y', [(i, i ^ 1) for i in range(4)])]
    pallas_call x21 -> x19, Pallas kernels: 15 us -> 15.4 us  [call(): pl.pallas_call(kernel, out_shape=outs, in_specs=[SM] * n_smem + [VM] * (l...]
  transfers between devices with their start and end apart: 26 -> 20, of which waited for: 14 -> 15; matrix products, arithmetic and copies ran while one was open for 0% -> 0% of each run, Pallas kernels for 9% -> 8%
where the time goes in v3:
time: 101 us
  waiting for transfers between devices  36.2 us (36%)
  starting transfers between devices  29.2 us (29%)
  Pallas kernels  15.6 us (15%)
  blocking collectives  14.4 us (14%)
  local copies, waits for them, and re-layouts  4.48 us (4%)
    ppermute x9, waiting for transfers between devices, along_z(): return lax.ppermute(array, SEQ, pairs)  21.3 us
    pallas_call x19, Pallas kernels, call(): pl.pallas_call(kernel, out_shape=outs, in_specs=[SM] * n_smem + [VM] * (l...  15.4 us
    all_to_all x1, blocking collectives, body(): got = lax.all_to_all(send, ('xl',) + FSDP, 0, 0, tiled=False)  14.4 us
    ppermute x9, starting transfers between devices, along_z(): return lax.ppermute(array, SEQ, pairs)  9.56 us
    ppermute x1, starting transfers between devices, body(): state = (keep_h, lax.ppermute(out_h, 'c', SWAP))  8.24 us
    ppermute x2, starting transfers between devices, core_sum(): got = lax.ppermute(send, 'c', SWAP)  4.86 us
    unnamed x24, local copies, waits for them, and re-layouts  4.48 us
    ppermute x1, waiting for transfers between devices, body(): back_q = lax.ppermute(out_q, 'xl', SWAP)  3.61 us
  transfers between devices with their start and end apart: 20, of which 15 were waited for; matrix products, arithmetic and copies ran while one was open for 0% of the time, Pallas kernels for 8%

profile of v3, /device:TPU:1, one launch (start us, length us, event | category | flops | bytes accessed | tf_op | source)
XLA Modules:
  0.0 100.8 jit_solution(9089569669049977830)
XLA Ops:
  2.3 14.4 %all_to_all.5.rec_ref = bf16[16,36,128]{2,1,0:T(8,128)(2,1)S(1)} all-to-all(bf16[16,36,128]{2,1,0:T(8,128)(2,1)S(1)} %bitcast.4), channel_id=1, replica_groups=mesh['z'=8,'xl'=2,'c'=2,'xh'=2,'y'=4] {'xl','xh','y'}, dimensions={0} | all-to-all | bytes 294912 | tf_op jit(solution)/shard_map/all_to_all | solution.py:481
  16.8 5.7 %collective-permute-start = (bf16[2,288,128]{2,1,0:T(8,128)(2,1)S(1)}, bf16[2,288,128]{2,1,0:T(8,128)(2,1)S(1)}, u32[]{:S(2)}, u32[]{:S(2)}) collective-permute-start(bf16[2,288,128]{2,1,0:T(8,128)(2,1)S(1)} %rows.1.a), channel_id=1, source_target_pairs={{0,32},{8,232},{16,48},{24,248},{32,0},{40,72},{48,16},{56,88},{64... | collective-permute-start | bytes 442376 | tf_op jit(solution)/shard_map/ppermute | solution.py:448
  22.5 2.2 %copy-done.1 = bf16[256,8192]{1,0:T(8,128)(2,1)S(1)} copy-done((bf16[256,8192]{1,0:T(8,128)(2,1)S(1)}, bf16[256,8192]{1,0:T(8,128)(2,1)}, u32[]{:S(2)}) %copy-start.1) | copy-done | bytes 4194328
  25.7 2.7 %local_prev.1 = (f32[528,128]{1,0:T(8,128)S(1)}, bf16[528,128]{1,0:T(8,128)(2,1)S(1)}, f32[256,128]{1,0:T(8,128)S(1)}, f32[16,256]{1,0:T(8,128)S(1)}, f32[16,256]{1,0:T(8,128)S(1)}, /*index=5*/f32[256,128]{1,0:T(8,128)S(1)}) custom-call(s32[4]{0:T(128)S(1)} %copy-done.9, f32[16,256]{1,0:T(8,128)S(1)} %bitcast.5, f32[1,128]{1,0:T(1,128)S(1)} %bitcast.6, ...), custom_call_target="tpu_custom_call" | custom-call | flops 30000000 | bytes 300000 | tf_op jit(solution)/shard_map/local_prev/pallas_call | solution.py:23
  28.7 3.3 %collective-permute-start.3 = (bf16[528,128]{1,0:T(8,128)(2,1)S(1)}, bf16[528,128]{1,0:T(8,128)(2,1)S(1)}, u32[]{:S(2)}, u32[]{:S(2)}) collective-permute-start(bf16[528,128]{1,0:T(8,128)(2,1)S(1)} %get-tuple-element.37), channel_id=1, source_target_pairs={{0,8},{8,0},{1,9},{9,1},{2,10},{10,2},{3,11},{11,3},{4,12},{12,4},... | collective-permute-start | bytes 405512 | tf_op jit(solution)/shard_map/ppermute | solution.py:452
  33.0 1.5 %collective-permute-done.2.refs_3_ = bf16[4,288,128]{2,1,0:T(8,128)(2,1)S(1)} collective-permute-done((bf16[4,288,128]{2,1,0:T(8,128)(2,1)S(1)}, bf16[4,288,128]{2,1,0:T(8,128)(2,1)S(1)}, u32[]{:S(2)}, u32[]{:S(2)}) %collective-permute-start.2) | collective-permute-done | bytes 294944 | tf_op jit(solution)/shard_map/ppermute | solution.py:448
  34.5 2.5 %collective-permute-start.4 = (bf16[4,288,128]{2,1,0:T(8,128)(2,1)S(1)}, bf16[4,288,128]{2,1,0:T(8,128)(2,1)S(1)}, u32[]{:S(2)}, u32[]{:S(2)}) collective-permute-start(bf16[4,288,128]{2,1,0:T(8,128)(2,1)S(1)} %collective-permute-done.2.refs_3_), channel_id=1, source_target_pairs={{0,8},{8,0},{1,9},{9,1},{2,10},{10,2},{3,11},{11,3},{4,12},{12,4},... | collective-permute-start | bytes 884744 | tf_op jit(solution)/shard_map/ppermute | solution.py:503
  37.0 2.6 %collective-permute-start.5 = (bf16[4,288,128]{2,1,0:T(8,128)(2,1)S(1)}, bf16[4,288,128]{2,1,0:T(8,128)(2,1)S(1)}, u32[]{:S(2)}, u32[]{:S(2)}) collective-permute-start(bf16[4,288,128]{2,1,0:T(8,128)(2,1)S(1)} %collective-permute-done.2.refs_3_), channel_id=1, source_target_pairs={{0,32},{8,232},{16,48},{24,248},{32,0},{40,72},{48,16},{56,88},{64... | collective-permute-start | bytes 884744 | tf_op jit(solution)/shard_map/ppermute | solution.py:448
  39.9 3.2 %collective-permute-done.6.got.got_p = bf16[272,128]{1,0:T(8,128)(2,1)S(1)} collective-permute-done((bf16[272,128]{1,0:T(8,128)(2,1)S(1)}, bf16[272,128]{1,0:T(8,128)(2,1)S(1)}, u32[]{:S(2)}, u32[]{:S(2)}) %collective-permute-start.6) | collective-permute-done | bytes 69664 | tf_op jit(solution)/shard_map/ppermute | solution.py:504
  44.0 2.0 %inside_prev.1.base_ref = f32[256,1024]{1,0:T(8,128)S(1)} custom-call(s32[4]{0:T(128)S(1)} %copy-done.9, f32[128]{0:T(128)S(1)} %copy-done.10, f32[256,128]{1,0:T(8,128)S(1)} %get-tuple-element.44.cum_ref, f32[16,256]{1,0:T(8,128)S(1)} %get-tuple-element.45.cumt_ref, f32[16,256]{1,0:T(8,128)S(1)} %get-tuple-element.46.dtt_ref, ...), custom_call_target="tpu_custom_call" | custom-call | flops 30000000 | bytes 300000 | tf_op jit(solution)/shard_map/inside_prev/pallas_call | solution.py:23
  46.6 3.3 %collective-permute-done.8.refs_2_ = bf16[4,288,128]{2,1,0:T(8,128)(2,1)S(1)} collective-permute-done((bf16[4,288,128]{2,1,0:T(8,128)(2,1)S(1)}, bf16[4,288,128]{2,1,0:T(8,128)(2,1)S(1)}, u32[]{:S(2)}, u32[]{:S(2)}) %collective-permute-start.8) | collective-permute-done | bytes 294944 | tf_op jit(solution)/shard_map/ppermute | solution.py:448
  49.9 2.5 %collective-permute-start.9 = (bf16[4,288,128]{2,1,0:T(8,128)(2,1)S(1)}, bf16[4,288,128]{2,1,0:T(8,128)(2,1)S(1)}, u32[]{:S(2)}, u32[]{:S(2)}) collective-permute-start(bf16[4,288,128]{2,1,0:T(8,128)(2,1)S(1)} %collective-permute-done.8.refs_2_), channel_id=1, source_target_pairs={{0,8},{8,0},{1,9},{9,1},{2,10},{10,2},{3,11},{11,3},{4,12},{12,4},... | collective-permute-start | bytes 884744 | tf_op jit(solution)/shard_map/ppermute | solution.py:513
  54.7 2.9 %collective-permute-done.10.pair_ref = bf16[256,128]{1,0:T(8,128)(2,1)S(1)} collective-permute-done((bf16[256,128]{1,0:T(8,128)(2,1)S(1)}, bf16[256,128]{1,0:T(8,128)(2,1)S(1)}, u32[]{:S(2)}, u32[]{:S(2)}) %collective-permute-start.10) | collective-permute-done | bytes 65568 | tf_op jit(solution)/shard_map/ppermute | solution.py:516
  57.6 2.7 %local_next.1 = (f32[528,128]{1,0:T(8,128)S(1)}, bf16[528,128]{1,0:T(8,128)(2,1)S(1)}, f32[256,128]{1,0:T(8,128)S(1)}, f32[16,256]{1,0:T(8,128)S(1)}, f32[16,256...) custom-call(s32[4]{0:T(128)S(1)} %copy-done.8, ...), custom_call_target="tpu_custom_call" | custom-call | flops 30000000 | bytes 300000 | tf_op jit(solution)/shard_map/local_next/pallas_call | solution.py:23
  60.3 1.6 %collective-permute-start.11 = (bf16[528,128]{1,0:T(8,128)(2,1)S(1)}, bf16[528,128]{1,0:T(8,128)(2,1)S(1)}, u32[]{:S(2)}, u32[]{:S(2)}) collective-permute-start(bf16[528,128]{1,0:T(8,128)(2,1)S(1)} %get-tuple-element.57), channel_id=1, source_target_pairs={{0,8},{8,0},{1,9},{9,1},{2,10},{10,2},{3,11},{11,3},{4,12},{12,4},... | collective-permute-start | bytes 405512 | tf_op jit(solution)/shard_map/ppermute | solution.py:452
  63.4 2.0 %inside_next.1.base_ref = f32[256,1024]{1,0:T(8,128)S(1)} custom-call(s32[4]{0:T(128)S(1)} %copy-done.8, f32[128]{0:T(128)S(1)} %copy-done.10, f32[256,128]{1,0:T(8,128)S(1)} %get-tuple-element.50.cum_ref, f32[16,256]{1,0:T(8,128)S(1)} %get-tuple-element.51.cumt_ref, f32[16,256]{1,0:T(8,128)S(1)} %get-tuple-element.52.dtt_ref, ...), custom_call_target="tpu_custom_call" | custom-call | flops 30000000 | bytes 300000 | tf_op jit(solution)/shard_map/inside_next/pallas_call | solution.py:23
  66.7 3.5 %collective-permute-done.13.got = bf16[2,272,128]{2,1,0:T(8,128)(2,1)S(1)} collective-permute-done((bf16[2,272,128]{2,1,0:T(8,128)(2,1)S(1)}, bf16[2,272,128]{2,1,0:T(8,128)(2,1)S(1)}, u32[]{:S(2)}, u32[]{:S(2)}) %collective-permute-start.13) | collective-permute-done | bytes 139296 | tf_op jit(solution)/shard_map/ppermute | solution.py:448
  70.5 3.1 %collective-permute-done.14.m2 = bf16[272,128]{1,0:T(8,128)(2,1)S(1)} collective-permute-done((bf16[272,128]{1,0:T(8,128)(2,1)S(1)}, bf16[272,128]{1,0:T(8,128)(2,1)S(1)}, u32[]{:S(2)}, u32[]{:S(2)}) %collective-permute-start.14) | collective-permute-done | bytes 69664 | tf_op jit(solution)/shard_map/ppermute | solution.py:448
  74.0 3.8 %collective-permute-done.15.m3 = bf16[272,128]{1,0:T(8,128)(2,1)S(1)} collective-permute-done((bf16[272,128]{1,0:T(8,128)(2,1)S(1)}, bf16[272,128]{1,0:T(8,128)(2,1)S(1)}, u32[]{:S(2)}, u32[]{:S(2)}) %collective-permute-start.15) | collective-permute-done | bytes 69664 | tf_op jit(solution)/shard_map/ppermute | solution.py:448
  77.7 3.2 %collective-permute-done.16.m4 = bf16[272,128]{1,0:T(8,128)(2,1)S(1)} collective-permute-done((bf16[272,128]{1,0:T(8,128)(2,1)S(1)}, bf16[272,128]{1,0:T(8,128)(2,1)S(1)}, u32[]{:S(2)}, u32[]{:S(2)}) %collective-permute-start.16) | collective-permute-done | bytes 69664 | tf_op jit(solution)/shard_map/ppermute | solution.py:448
  81.1 2.9 %collective-permute-done.17.m5 = bf16[272,128]{1,0:T(8,128)(2,1)S(1)} collective-permute-done((bf16[272,128]{1,0:T(8,128)(2,1)S(1)}, bf16[272,128]{1,0:T(8,128)(2,1)S(1)}, u32[]{:S(2)}, u32[]{:S(2)}) %collective-permute-start.17) | collective-permute-done | bytes 69664 | tf_op jit(solution)/shard_map/ppermute | solution.py:448
  84.6 3.6 %collective-permute-done.18.other = bf16[2,256,128]{2,1,0:T(8,128)(2,1)S(1)} collective-permute-done((bf16[2,256,128]{2,1,0:T(8,128)(2,1)S(1)}, bf16[2,256,128]{2,1,0:T(8,128)(2,1)S(1)}, u32[]{:S(2)}, u32[]{:S(2)}) %collective-permute-start.18) | collective-permute-done | bytes 131104 | tf_op jit(solution)/shard_map/ppermute | solution.py:531
  88.5 8.2 %collective-permute-start.19 = (bf16[2,512,128]{2,1,0:T(8,128)(2,1)S(1)}, bf16[2,512,128]{2,1,0:T(8,128)(2,1)S(1)}, u32[]{:S(2)}, u32[]{:S(2)}) collective-permute-start(bf16[2,512,128]{2,1,0:T(8,128)(2,1)S(1)} %get-tuple-element.66), channel_id=1, source_target_pairs={{0,8},{8,0},{1,9},{9,1},{2,10},{10,2},{3,11},{11,3},{4,12},{12,4},... | collective-permute-start | bytes 786440 | tf_op jit(solution)/shard_map/ppermute | solution.py:535
  99.3 1.5 %final_next.1 = bf16[256,1024]{1,0:T(8,128)(2,1)} custom-call(f32[256,1024]{1,0:T(8,128)S(1)} %inside_next.1.base_ref, f32[256,128]{1,0:T(8,128)S(1)} %get-tuple-element.55.late_ref, bf16[2,512,128]{2,1,0:T(8,128)(2,1)S(1)} %get-tuple-element.65.keep_ref, bf16[2,512,128]{2,1,0:T(8,128)(2,1)S(1)} %collective-permute-done.19.got_ref, ...), custom_call_target="tpu_custom_call" | custom-call | flops 20000000 | bytes 200000 | tf_op jit(solution)/shard_map/final_next/pallas_call | solution.py:23
  (61 shorter events, 15.1 us)
Async XLA Ops:
  16.8 11.6 %collective-permute-start = (bf16[2,288,128]{2,1,0:T(8,128)(2,1)S(1)}, bf16[2,288,128]{2,1,0:T(8,128)(2,1)S(1)}, u32[]{:S(2)}, u32[]{:S(2)}) collective-permute-start(bf16[2,288,128]{2,1,0:T(8,128)(2,1)S(1)} %rows.1.a), channel_id=1, source_target_pairs={{0,32},{8,232},{16,48},{24,248},{32,0},{40,72},{48,16},{56,88},{64... | collective-permute-start | bytes 442376 | tf_op jit(solution)/shard_map/ppermute | solution.py:448
  25.0 19.0 %copy-start.10 = (f32[128]{0:T(128)S(1)}, f32[128]{0:T(128)}, u32[]{:S(2)}) copy-start(f32[128]{0:T(128)} %skip.3) | copy-start | bytes 1540
  28.5 4.6 %collective-permute-start.1 = (bf16[4,288,128]{2,1,0:T(8,128)(2,1)S(1)}, bf16[4,288,128]{2,1,0:T(8,128)(2,1)S(1)}, u32[]{:S(2)}, u32[]{:S(2)}) collective-permute-start(bf16[4,288,128]{2,1,0:T(8,128)(2,1)S(1)} %pack.1.refs_1_), channel_id=1, source_target_pairs={{0,8},{8,0},{1,9},{9,1},{2,10},{10,2},{3,11},{11,3},{4,12},{12,4},... | collective-permute-start | bytes 884744 | tf_op jit(solution)/shard_map/ppermute | solution.py:499
  28.6 6.0 %collective-permute-start.2 = (bf16[4,288,128]{2,1,0:T(8,128)(2,1)S(1)}, bf16[4,288,128]{2,1,0:T(8,128)(2,1)S(1)}, u32[]{:S(2)}, u32[]{:S(2)}) collective-permute-start(bf16[4,288,128]{2,1,0:T(8,128)(2,1)S(1)} %pack.1.refs_1_), channel_id=1, source_target_pairs={{0,224},{8,40},{16,240},{24,56},{32,64},{40,8},{48,80},{56,24},{64... | collective-permute-start | bytes 884744 | tf_op jit(solution)/shard_map/ppermute | solution.py:448
  28.7 4.3 %collective-permute-start.3 = (bf16[528,128]{1,0:T(8,128)(2,1)S(1)}, bf16[528,128]{1,0:T(8,128)(2,1)S(1)}, u32[]{:S(2)}, u32[]{:S(2)}) collective-permute-start(bf16[528,128]{1,0:T(8,128)(2,1)S(1)} %get-tuple-element.37), channel_id=1, source_target_pairs={{0,8},{8,0},{1,9},{9,1},{2,10},{10,2},{3,11},{11,3},{4,12},{12,4},... | collective-permute-start | bytes 405512 | tf_op jit(solution)/shard_map/ppermute | solution.py:452
  34.5 8.6 %collective-permute-start.4 = (bf16[4,288,128]{2,1,0:T(8,128)(2,1)S(1)}, bf16[4,288,128]{2,1,0:T(8,128)(2,1)S(1)}, u32[]{:S(2)}, u32[]{:S(2)}) collective-permute-start(bf16[4,288,128]{2,1,0:T(8,128)(2,1)S(1)} %collective-permute-done.2.refs_3_), channel_id=1, source_target_pairs={{0,8},{8,0},{1,9},{9,1},{2,10},{10,2},{3,11},{11,3},{4,12},{12,4},... | collective-permute-start | bytes 884744 | tf_op jit(solution)/shard_map/ppermute | solution.py:503
  37.0 6.8 %collective-permute-start.5 = (bf16[4,288,128]{2,1,0:T(8,128)(2,1)S(1)}, bf16[4,288,128]{2,1,0:T(8,128)(2,1)S(1)}, u32[]{:S(2)}, u32[]{:S(2)}) collective-permute-start(bf16[4,288,128]{2,1,0:T(8,128)(2,1)S(1)} %collective-permute-done.2.refs_3_), channel_id=1, source_target_pairs={{0,32},{8,232},{16,48},{24,248},{32,0},{40,72},{48,16},{56,88},{64... | collective-permute-start | bytes 884744 | tf_op jit(solution)/shard_map/ppermute | solution.py:448
  39.6 3.5 %collective-permute-start.6 = (bf16[272,128]{1,0:T(8,128)(2,1)S(1)}, bf16[272,128]{1,0:T(8,128)(2,1)S(1)}, u32[]{:S(2)}, u32[]{:S(2)}) collective-permute-start(bf16[272,128]{1,0:T(8,128)(2,1)S(1)} %get-tuple-element.40), channel_id=1, source_target_pairs={{0,16},{16,0},{1,17},{17,1},{2,18},{18,2},{3,19},{19,3},{4,20},{20... | collective-permute-start | bytes 208904 | tf_op jit(solution)/shard_map/ppermute | solution.py:504
  43.8 2.3 %collective-permute-start.7 = (bf16[4,288,128]{2,1,0:T(8,128)(2,1)S(1)}, bf16[4,288,128]{2,1,0:T(8,128)(2,1)S(1)}, u32[]{:S(2)}, u32[]{:S(2)}) collective-permute-start(bf16[4,288,128]{2,1,0:T(8,128)(2,1)S(1)} %collective-permute-done.5.refs_2_), channel_id=1, source_target_pairs={{0,8},{8,0},{1,9},{9,1},{2,10},{10,2},{3,11},{11,3},{4,12},{12,4},... | collective-permute-start | bytes 884744 | tf_op jit(solution)/shard_map/ppermute | solution.py:509
  43.9 6.0 %collective-permute-start.8 = (bf16[4,288,128]{2,1,0:T(8,128)(2,1)S(1)}, bf16[4,288,128]{2,1,0:T(8,128)(2,1)S(1)}, u32[]{:S(2)}, u32[]{:S(2)}) collective-permute-start(bf16[4,288,128]{2,1,0:T(8,128)(2,1)S(1)} %collective-permute-done.5.refs_2_), channel_id=1, source_target_pairs={{0,224},{8,40},{16,240},{24,56},{32,64},{40,8},{48,80},{56,24},{64... | collective-permute-start | bytes 884744 | tf_op jit(solution)/shard_map/ppermute | solution.py:448
  46.1 11.5 %copy-start.2 = (bf16[256,1024]{1,0:T(8,128)(2,1)S(1)}, bf16[256,1024]{1,0:T(8,128)(2,1)}, u32[]{:S(2)}) copy-start(bf16[256,1024]{1,0:T(8,128)(2,1)} %val_ref.7) | copy-start | bytes 1572868
  46.1 11.5 %copy-start.8 = (s32[4]{0:T(128)S(1)}, s32[4]{0:T(128)}, u32[]{:S(2)}) copy-start(s32[4]{0:T(128)} %sc.6) | copy-start | bytes 52
  46.1 11.5 %copy-start.11 = (f32[128]{0:T(128)S(1)}, f32[128]{0:T(128)}, u32[]{:S(2)}) copy-start(f32[128]{0:T(128)} %param.17) | copy-start | bytes 1540
  49.9 3.7 %collective-permute-start.9 = (bf16[4,288,128]{2,1,0:T(8,128)(2,1)S(1)}, bf16[4,288,128]{2,1,0:T(8,128)(2,1)S(1)}, u32[]{:S(2)}, u32[]{:S(2)}) collective-permute-start(bf16[4,288,128]{2,1,0:T(8,128)(2,1)S(1)} %collective-permute-done.8.refs_2_), channel_id=1, source_target_pairs={{0,8},{8,0},{1,9},{9,1},{2,10},{10,2},{3,11},{11,3},{4,12},{12,4},... | collective-permute-start | bytes 884744 | tf_op jit(solution)/shard_map/ppermute | solution.py:513
  54.2 3.4 %collective-permute-start.10 = (bf16[256,128]{1,0:T(8,128)(2,1)S(1)}, bf16[256,128]{1,0:T(8,128)(2,1)S(1)}, u32[]{:S(2)}, u32[]{:S(2)}) collective-permute-start(bf16[256,128]{1,0:T(8,128)(2,1)S(1)} %get-tuple-element.49.mine_ref), channel_id=1, source_target_pairs={{0,1},{1,0},{2,3},{3,2},{4,5},{5,4},{6,7},{7,6},{8,9},{9,8},{10,11... | collective-permute-start | bytes 196616 | tf_op jit(solution)/shard_map/ppermute | solution.py:516
  60.3 2.6 %collective-permute-start.11 = (bf16[528,128]{1,0:T(8,128)(2,1)S(1)}, bf16[528,128]{1,0:T(8,128)(2,1)S(1)}, u32[]{:S(2)}, u32[]{:S(2)}) collective-permute-start(bf16[528,128]{1,0:T(8,128)(2,1)S(1)} %get-tuple-element.57), channel_id=1, source_target_pairs={{0,8},{8,0},{1,9},{9,1},{2,10},{10,2},{3,11},{11,3},{4,12},{12,4},... | collective-permute-start | bytes 405512 | tf_op jit(solution)/shard_map/ppermute | solution.py:452
  63.0 3.2 %collective-permute-start.12 = (bf16[272,128]{1,0:T(8,128)(2,1)S(1)}, bf16[272,128]{1,0:T(8,128)(2,1)S(1)}, u32[]{:S(2)}, u32[]{:S(2)}) collective-permute-start(bf16[272,128]{1,0:T(8,128)(2,1)S(1)} %get-tuple-element.59), channel_id=1, source_target_pairs={{0,16},{16,0},{1,17},{17,1},{2,18},{18,2},{3,19},{19,3},{4,20},{20... | collective-permute-start | bytes 208904 | tf_op jit(solution)/shard_map/ppermute | solution.py:521
  66.3 4.0 %collective-permute-start.13 = (bf16[2,272,128]{2,1,0:T(8,128)(2,1)S(1)}, bf16[2,272,128]{2,1,0:T(8,128)(2,1)S(1)}, u32[]{:S(2)}, u32[]{:S(2)}) collective-permute-start(bf16[2,272,128]{2,1,0:T(8,128)(2,1)S(1)} %get-tuple-element.61), channel_id=1, source_target_pairs={{0,32},{8,24},{16,48},{24,8},{32,0},{40,72},{48,16},{56,88},{64,96... | collective-permute-start | bytes 417800 | tf_op jit(solution)/shard_map/ppermute | solution.py:448
  70.4 3.2 %collective-permute-start.14 = (bf16[272,128]{1,0:T(8,128)(2,1)S(1)}, bf16[272,128]{1,0:T(8,128)(2,1)S(1)}, u32[]{:S(2)}, u32[]{:S(2)}) collective-permute-start(bf16[272,128]{1,0:T(8,128)(2,1)S(1)} %pairs.1), channel_id=1, source_target_pairs={{0,16},{8,40},{16,0},{24,56},{32,64},{40,8},{48,80},{56,24},{64,32... | collective-permute-start | bytes 208904 | tf_op jit(solution)/shard_map/ppermute | solution.py:448
  73.6 4.1 %collective-permute-start.15 = (bf16[272,128]{1,0:T(8,128)(2,1)S(1)}, bf16[272,128]{1,0:T(8,128)(2,1)S(1)}, u32[]{:S(2)}, u32[]{:S(2)}) collective-permute-start(bf16[272,128]{1,0:T(8,128)(2,1)S(1)} %collective-permute-done.14.m2), channel_id=1, source_target_pairs={{0,32},{8,24},{16,48},{24,8},{32,0},{40,72},{48,16},{56,88},{64,96... | collective-permute-start | bytes 208904 | tf_op jit(solution)/shard_map/ppermute | solution.py:448
  77.7 3.2 %collective-permute-start.16 = (bf16[272,128]{1,0:T(8,128)(2,1)S(1)}, bf16[272,128]{1,0:T(8,128)(2,1)S(1)}, u32[]{:S(2)}, u32[]{:S(2)}) collective-permute-start(bf16[272,128]{1,0:T(8,128)(2,1)S(1)} %collective-permute-done.15.m3), channel_id=1, source_target_pairs={{0,16},{8,40},{16,0},{24,56},{32,64},{40,8},{48,80},{56,24},{64,32... | collective-permute-start | bytes 208904 | tf_op jit(solution)/shard_map/ppermute | solution.py:448
  80.9 3.2 %collective-permute-start.17 = (bf16[272,128]{1,0:T(8,128)(2,1)S(1)}, bf16[272,128]{1,0:T(8,128)(2,1)S(1)}, u32[]{:S(2)}, u32[]{:S(2)}) collective-permute-start(bf16[272,128]{1,0:T(8,128)(2,1)S(1)} %collective-permute-done.16.m4), channel_id=1, source_target_pairs={{0,32},{8,24},{16,48},{24,8},{32,0},{40,72},{48,16},{56,88},{64,96... | collective-permute-start | bytes 208904 | tf_op jit(solution)/shard_map/ppermute | solution.py:448
  84.3 3.9 %collective-permute-start.18 = (bf16[2,256,128]{2,1,0:T(8,128)(2,1)S(1)}, bf16[2,256,128]{2,1,0:T(8,128)(2,1)S(1)}, u32[]{:S(2)}, u32[]{:S(2)}) collective-permute-start(bf16[2,256,128]{2,1,0:T(8,128)(2,1)S(1)} %get-tuple-element.64), channel_id=1, source_target_pairs={{0,16},{16,0},{1,17},{17,1},{2,18},{18,2},{3,19},{19,3},{4,20},{20... | collective-permute-start | bytes 393224 | tf_op jit(solution)/shard_map/ppermute | solution.py:531
  88.5 9.4 %collective-permute-start.19 = (bf16[2,512,128]{2,1,0:T(8,128)(2,1)S(1)}, bf16[2,512,128]{2,1,0:T(8,128)(2,1)S(1)}, u32[]{:S(2)}, u32[]{:S(2)}) collective-permute-start(bf16[2,512,128]{2,1,0:T(8,128)(2,1)S(1)} %get-tuple-element.66), channel_id=1, source_target_pairs={{0,8},{8,0},{1,9},{9,1},{2,10},{10,2},{3,11},{11,3},{4,12},{12,4},... | collective-permute-start | bytes 786440 | tf_op jit(solution)/shard_map/ppermute | solution.py:535
  (8 other events, 16.1 us)
